TPU v7x, 8 devices: a whole 2x2x1 slice. The times are simulated.
8 devices in a mesh: rep: 2 (over y, z), dp: 4 (over x, core).
Axes of the slice: x: 2, y: 2, z: 1, core: 2. Of those that a mesh axis runs over, the one named last changes fastest.
Arguments:
- x: bfloat16 [8, 2048, 896], P(('rep', 'dp')), parts along dimension 0
- dy: bfloat16 [8, 2048, 896], P(('rep', 'dp')), parts along dimension 0
- w_gate: bfloat16 [2, 896, 2560], replicated
- w_up: bfloat16 [2, 896, 2560], replicated
- w_down: bfloat16 [2, 2560, 896], replicated
- m_w_gate: float32 [2, 896, 2560], P(None, 'dp')
- m_w_up: float32 [2, 896, 2560], P(None, 'dp')
- m_w_down: float32 [2, 2560, 896], P(None, 'dp')
- v_w_gate: float32 [2, 896, 2560], P(None, 'dp')
- v_w_up: float32 [2, 896, 2560], P(None, 'dp')
- v_w_down: float32 [2, 2560, 896], P(None, 'dp')
Outputs:
- output 1: bfloat16 [4, 896, 2560], P('rep'), parts along dimension 0
- output 2: bfloat16 [4, 896, 2560], P('rep'), parts along dimension 0
- output 3: bfloat16 [4, 2560, 896], P('rep'), parts along dimension 0
- output 4: float32 [4, 896, 2560], P('rep', 'dp'), parts along dimension 0
- output 5: float32 [4, 896, 2560], P('rep', 'dp'), parts along dimension 0
- output 6: float32 [4, 2560, 896], P('rep', 'dp'), parts along dimension 0
- output 7: float32 [4, 896, 2560], P('rep', 'dp'), parts along dimension 0
- output 8: float32 [4, 896, 2560], P('rep', 'dp'), parts along dimension 0
- output 9: float32 [4, 2560, 896], P('rep', 'dp'), parts along dimension 0
There are 2 independent parts. A program takes and returns all parts, laid end to end along the dimension named above; an argument that names none is the same for every part.
All inputs are finite; a program needn't handle non-finite values.
Results may differ from a plain program's by a relative error of at most 0.022.
Values are sent between devices in bfloat16 or wider.
A program may use at most 2 GiB of HBM per device.

v0:
```python
import jax
import jax.numpy as jnp
from jax import lax
from jax.experimental import pallas as pl
from jax.experimental.pallas import tpu as pltpu
from jax.sharding import PartitionSpec as P


T, D, FF = 2048, 896, 2560
GROUP = 4
OWN_D, OWN_F = D // GROUP, FF // GROUP
CHUNKS, PIECE = 5, 128
C = GROUP * PIECE
TILE = 512
TILES = T // TILE
BF, F32 = jnp.bfloat16, jnp.float32
ANY = pl.BlockSpec(memory_space=pl.ANY)


def dot(a, b, over=(1, 0)):
    return lax.dot_general(a, b, (((over[0],), (over[1],)), ((), ())), preferred_element_type=F32)


def logistic(x):
    return 1.0 / (1.0 + jnp.exp(-x))


def normed(h):
    wide = h.astype(F32)
    return (wide * lax.rsqrt(jnp.mean(wide * wide, -1, keepdims=True) + 1e-6)).astype(BF)


def at(i, size):
    return pl.ds(pl.multiple_of(i * size, size), size)


def hidden(d, k):
    return pl.ds(pl.multiple_of(d * OWN_F + k * PIECE, PIECE), PIECE)


def forward_kernel(x, wg, wu, wd, s_out, q_out, p_out, h_out, a_out, at_out, a0t_out, wgs, wus, wds, p, sem):
    t = pl.program_id(0)

    def copies(k):
        for d in range(GROUP):
            yield pltpu.make_async_copy(wg.at[0, :, hidden(d, k)], wgs.at[k, :, at(d, PIECE)], sem.at[k, d])
            yield pltpu.make_async_copy(wu.at[0, :, hidden(d, k)], wus.at[k, :, at(d, PIECE)], sem.at[k, 4 + d])
        for d in range(GROUP):
            yield pltpu.make_async_copy(wd.at[0, hidden(d, k), :], wds.at[at(k * GROUP + d, PIECE), :], sem.at[k, 8 + d])

    @pl.when(t == 0)
    def _():
        @pl.loop(0, CHUNKS)
        def _(k):
            for c in copies(k):
                c.start()

    a = normed(x[0])
    a0t_out[...] = a.T

    @pl.loop(0, CHUNKS)
    def _(k):
        @pl.when(t == 0)
        def _():
            for c in copies(k):
                c.wait()

        gate = dot(a, wgs[k])
        up = dot(a, wus[k])
        s = logistic(gate)
        silu = gate * s
        prod = (silu * up).astype(BF)
        s_out[k] = silu
        q_out[k] = up * (s * (1.0 + gate * (1.0 - s)))
        p_out[k] = prod
        p[:, at(k, C)] = prod

    h = (x[0].astype(F32) + dot(p[...], wds[...]).astype(BF).astype(F32)).astype(BF)
    h_out[...] = h
    a = normed(h)
    a_out[...] = a
    at_out[...] = a.T


def forward(x, wg, wu, wd):
    wide = jax.ShapeDtypeStruct((CHUNKS, T, C), F32)
    rows = jax.ShapeDtypeStruct((T, D), BF)
    turned = jax.ShapeDtypeStruct((D, T), BF)
    block = pl.BlockSpec((CHUNKS, TILE, C), lambda t: (0, t, 0))
    row_block = pl.BlockSpec((TILE, D), lambda t: (t, 0))
    turned_block = pl.BlockSpec((D, TILE), lambda t: (0, t))
    return pl.pallas_call(
        forward_kernel,
        grid=(TILES,),
        out_shape=[wide, wide, jax.ShapeDtypeStruct((CHUNKS, T, C), BF), rows, rows, turned, turned],
        in_specs=[pl.BlockSpec((1, TILE, D), lambda t: (0, t, 0)), ANY, ANY, ANY],
        out_specs=[block, block, block, row_block, row_block, turned_block, turned_block],
        scratch_shapes=[
            pltpu.VMEM((CHUNKS, D, C), BF),
            pltpu.VMEM((CHUNKS, D, C), BF),
            pltpu.VMEM((FF, D), BF),
            pltpu.VMEM((TILE, FF), BF),
            pltpu.SemaphoreType.DMA((CHUNKS, 12)),
        ],
        compiler_params=pltpu.CompilerParams(vmem_limit_bytes=64_000_000),
        cost_estimate=pl.CostEstimate(flops=6 * T * D * FF, bytes_accessed=80_000_000, transcendentals=T * FF),
        name="forward",
    )(x, wg, wu, wd)


def backward_kernel(
    a1, a1t, dy, h1, a0t, s0, q0, p0, wg, wu, wd,
    gg, gu, gd, ss,
    a, atr, dh, h, pr, dg, du, da, wgv, wuv, wdv, dwg, dwd, rdg, rdd, isg, isd, irg, ird, owng, ownd, ssg, ssd, nsend, nrecv,
    isem, wsem, psem, ssem, d2d_send, d2d_recv, ici_send, ici_recv, osem, n_send, n_recv,
):
    me = lax.axis_index("dp")
    core, chip = me % 2, me // 2
    other = 1 - chip
    near, far, across = me + 1 - 2 * core, (me + 2) % 4, 3 - me

    def remote(src, dst, send, recv, to):
        return pltpu.make_async_remote_copy(src, dst, send, recv, device_id={"dp": to}, device_id_type=pl.DeviceIdType.MESH)

    def weights(layer, k, slot, all_three):
        for d in range(GROUP):
            yield pltpu.make_async_copy(wd.at[layer, hidden(d, k), :], wdv.at[slot, at(d, PIECE), :], wsem.at[slot, d])
        if all_three:
            for d in range(GROUP):
                yield pltpu.make_async_copy(wg.at[layer, :, hidden(d, k)], wgv.at[slot, :, at(d, PIECE)], wsem.at[slot, 4 + d])
                yield pltpu.make_async_copy(wu.at[layer, :, hidden(d, k)], wuv.at[slot, :, at(d, PIECE)], wsem.at[slot, 8 + d])

    def start(copies):
        for c in copies:
            c.start()

    def wait(copies):
        for c in copies:
            c.wait()

    def rows_of(k):
        return [pltpu.make_async_copy(p0.at[k], pr.at[(k + 1) % 2], psem.at[(k + 1) % 2])]

    def saved(step):
        k, t, slot = step // TILES, step % TILES, step % 2
        for i, source in enumerate((s0, q0)):
            yield pltpu.make_async_copy(source.at[k, at(t, TILE), :], da.at[at(2 * i + slot, TILE), pl.ds(0, C)], ssem.at[slot, i])

    first = [pltpu.make_async_copy(src, dst, isem.at[i]) for i, (src, dst) in enumerate(((a1, a), (dy, dh), (a1t, atr), (h1, h)))]
    start(weights(1, 0, 0, True))
    start(first)
    start(rows_of(0))
    barrier = pltpu.get_barrier_semaphore()
    for to in (near, far, across):
        pl.semaphore_signal(barrier, inc=1, device_id={"dp": to}, device_id_type=pl.DeviceIdType.MESH)
    ssg[...] = jnp.zeros_like(ssg)
    ssd[...] = jnp.zeros_like(ssd)

    @pl.loop(0, TILES)
    def _(t):
        da[at(t, TILE), :] = jnp.zeros((TILE, D), F32)

    pl.semaphore_wait(barrier, 3)
    wait(first)

    def weight_gradients(slot):
        @pl.loop(0, 2)
        def _(half):
            down = dot(pr[slot, :, at(half, 2 * PIECE)], dh[...], (0, 0)).astype(BF)
            dwd[1 - core, half] = down[:PIECE]
            dwd[core, half] = down[PIECE:]
            turned = atr[at(half, 2 * OWN_D), :]
            for i, d in enumerate((dg, du)):
                out = dot(turned, d[...]).astype(BF)
                rows = slice(i * OWN_D, (i + 1) * OWN_D)
                dwg[1 - core, half, rows, :] = out[:OWN_D]
                dwg[core, half, rows, :] = out[OWN_D:]

    def to_near(n):
        return [
            remote(dwd.at[0], rdd.at[n % 2], d2d_send.at[0, n], d2d_recv.at[0, n], near),
            remote(dwg.at[0], rdg.at[n % 2], d2d_send.at[1, n], d2d_recv.at[1, n], near),
        ]

    def to_far(n):
        return [
            remote(isd.at[n % CHUNKS], ird.at[n], ici_send.at[0, n], ici_recv.at[0, n], far),
            remote(isg.at[n % CHUNKS], irg.at[n], ici_send.at[1, n], ici_recv.at[1, n], far),
        ]

    def sum_on_chip(n):
        slot, place = n % 2, n % CHUNKS
        near_copies, far_copies = to_near(n), to_far(n)
        for own, got, out, near_copy, far_copy in ((dwd, rdd, isd, near_copies[0], far_copies[0]), (dwg, rdg, isg, near_copies[1], far_copies[1])):
            near_copy.wait()
            out[place] = (own[1, other].astype(F32) + got[slot, other].astype(F32)).astype(BF)
            far_copy.start()
        ownd[place] = dwd[1, chip].astype(F32) + rdd[slot, chip].astype(F32)
        owng[place] = dwg[1, chip].astype(F32) + rdg[slot, chip].astype(F32)

    def results(n, layer, k):
        yield pltpu.make_async_copy(ird.at[n], gd.at[layer, at(k, PIECE), :], osem.at[n, 0])
        for i, out in enumerate((gg, gu)):
            for d in range(GROUP):
                yield pltpu.make_async_copy(
                    irg.at[n, pl.ds(i * OWN_D, OWN_D), at(d, PIECE)], out.at[layer, :, hidden(d, k)], osem.at[n, 1 + i * GROUP + d]
                )

    def finish(n, layer, k):
        place = n % CHUNKS
        for own, got, total, copy in ((ownd, ird, ssd, to_far(n)[0]), (owng, irg, ssg, to_far(n)[1])):
            copy.wait()
            g = (own[place] + got[n].astype(F32)).astype(BF)
            got[n] = g
            g = g.astype(F32)
            total[...] += jnp.sum((g * g).reshape(-1, 8, g.shape[-1]), 0)
        start(results(n, layer, k))

    @pl.loop(0, CHUNKS)
    def _(k):
        slot = k % 2
        wait(weights(1, k, slot, True))

        @pl.when(k < CHUNKS - 1)
        def _():
            start(weights(1, k + 1, 1 - slot, True))

        @pl.when(k == CHUNKS - 1)
        def _():
            start(weights(0, 0, CHUNKS % 2, False))

        @pl.loop(0, TILES)
        def _(t):
            r = at(t, TILE)
            x = a[r, :]
            gate = dot(x, wgv[slot])
            up = dot(x, wuv[slot])
            dp = dot(dh[r, :], wdv[slot], (1, 1)).astype(BF).astype(F32)
            s = logistic(gate)
            silu = gate * s
            pr[0, r, :] = (silu * up).astype(BF)
            dg[r, :] = (dp * (up * (s * (1.0 + gate * (1.0 - s))))).astype(BF)
            du[r, :] = (dp * silu).astype(BF)

        weight_gradients(0)
        start(to_near(k))

        @pl.loop(0, TILES)
        def _(t):
            r = at(t, TILE)
            da[r, :] += dot(dg[r, :], wgv[slot], (1, 1)) + dot(du[r, :], wuv[slot], (1, 1))

        sum_on_chip(k)

    turn = pltpu.make_async_copy(a0t, atr, isem.at[2])
    turn.start()

    @pl.loop(0, T // 256)
    def _(t):
        r = at(t, 256)
        wide = h[r, :].astype(F32)
        scale = lax.rsqrt(jnp.mean(wide * wide, -1, keepdims=True) + 1e-6)
        ct = da[r, :].astype(BF).astype(F32)
        back = scale * ct - wide * (scale * scale * scale * jnp.mean(wide * ct, -1, keepdims=True))
        dh[r, :] = (dh[r, :].astype(F32) + back.astype(BF).astype(F32)).astype(BF)

    start(saved(0))
    turn.wait()

    @pl.loop(0, CHUNKS)
    def _(k):
        n = CHUNKS + k
        slot = n % 2
        wait(weights(0, k, slot, False))
        wait(rows_of(k))

        @pl.when(k < CHUNKS - 1)
        def _():
            start(weights(0, k + 1, 1 - slot, False))
            start(rows_of(k + 1))

        @pl.loop(0, TILES)
        def _(t):
            r = at(t, TILE)
            step = k * TILES + t

            @pl.when(step < CHUNKS * TILES - 1)
            def _():
                start(saved(step + 1))

            dp = dot(dh[r, :], wdv[slot], (1, 1)).astype(BF).astype(F32)
            wait(saved(step))
            du[r, :] = (dp * da[at(step % 2, TILE), pl.ds(0, C)]).astype(BF)
            dg[r, :] = (dp * da[at(2 + step % 2, TILE), pl.ds(0, C)]).astype(BF)

        weight_gradients((k + 1) % 2)
        start(to_near(n))
        finish(k, 1, k)
        sum_on_chip(n)

    @pl.loop(0, CHUNKS)
    def _(k):
        finish(CHUNKS + k, 0, k)

    nsend[...] = jnp.full((8, 128), jnp.sum(ssg[...]) + jnp.sum(ssd[...]), F32)
    norms = [remote(nsend, nrecv.at[i], n_send.at[i], n_recv.at[i], to) for i, to in enumerate((near, far, across))]
    start(norms)

    @pl.loop(0, CHUNKS)
    def _(k):
        wait(results(k, 1, k))
        wait(results(CHUNKS + k, 0, k))

    wait(norms)
    ss[...] = nsend[...] + nrecv[0] + nrecv[1] + nrecv[2]


def backward(*args):
    vmem, sem = pltpu.VMEM, pltpu.SemaphoreType.DMA
    g_rows = 2 * OWN_D
    return pl.pallas_call(
        backward_kernel,
        out_shape=[
            jax.ShapeDtypeStruct((2, OWN_D, FF), BF),
            jax.ShapeDtypeStruct((2, OWN_D, FF), BF),
            jax.ShapeDtypeStruct((2, OWN_F, D), BF),
            jax.ShapeDtypeStruct((8, 128), F32),
        ],
        in_specs=[ANY] * 11,
        out_specs=[ANY] * 3 + [pl.BlockSpec(memory_space=pltpu.VMEM)],
        scratch_shapes=[
            vmem((T, D), BF), vmem((D, T), BF), vmem((T, D), BF), vmem((T, D), BF),
            vmem((2, T, C), BF), vmem((T, C), BF), vmem((T, C), BF), vmem((T, D), F32),
            vmem((2, D, C), BF), vmem((2, D, C), BF), vmem((2, C, D), BF),
            vmem((2, 2, g_rows, C), BF), vmem((2, 2, PIECE, D), BF),
            vmem((2, 2, g_rows, C), BF), vmem((2, 2, PIECE, D), BF),
            vmem((CHUNKS, g_rows, C), BF), vmem((CHUNKS, PIECE, D), BF),
            vmem((2 * CHUNKS, g_rows, C), BF), vmem((2 * CHUNKS, PIECE, D), BF),
            vmem((CHUNKS, g_rows, C), F32), vmem((CHUNKS, PIECE, D), F32),
            vmem((8, C), F32), vmem((8, D), F32), vmem((8, 128), F32), vmem((3, 8, 128), F32),
            sem((4,)), sem((2, 12)), sem((2,)), sem((2, 2)),
            sem((2, 2 * CHUNKS)), sem((2, 2 * CHUNKS)), sem((2, 2 * CHUNKS)), sem((2, 2 * CHUNKS)),
            sem((2 * CHUNKS, 9)), sem((3,)), sem((3,)),
        ],
        compiler_params=pltpu.CompilerParams(vmem_limit_bytes=67_000_000, collective_id=0, has_side_effects=True),
        cost_estimate=pl.CostEstimate(flops=24 * T * D * FF, bytes_accessed=130_000_000, transcendentals=T * FF),
        name="backward",
    )(*args)


def solution(mesh):
    far = [(d, d ^ 2) for d in range(GROUP)]
    near = [(d, d ^ 1) for d in range(GROUP)]

    def step(x, dy, *arrays):
        weights, ms, vs = (arrays[i : i + 3] for i in (0, 3, 6))
        me = lax.axis_index("dp")
        s0, q0, p0, h1, a1, a1t, a0t = forward(x, *weights)
        *gradients, squares = backward(a1, a1t, dy[0], h1, a0t, s0, q0, p0, *weights)
        count = sum(w.size for w in weights)
        factor = jnp.minimum(1.0, 0.5 * lax.rsqrt(squares[0, 0] / count + 1e-30))

        def adamw(w, m, v, g, factor):
            g = g.astype(F32) * factor
            m = 0.9 * m + 0.1 * g
            v = 0.95 * v + 0.05 * g * g
            return (w.astype(F32) - 0.02 * (m * lax.rsqrt(v + 1e-8) + 0.1 * w.astype(F32))).astype(BF), m, v

        mine = []
        for w, g in zip(weights, gradients, strict=True):
            mine.append(lax.dynamic_index_in_dim(w.reshape(g.shape[0], GROUP, *g.shape[1:]), me, 1, keepdims=False))
        units = [(i, layer) for i in range(3) for layer in range(2)]
        blocks = {}
        for i, layer in units:
            block = adamw(mine[i][layer], ms[i][layer], vs[i][layer], gradients[i][layer], factor)[0]
            block, factor = lax.optimization_barrier((block, factor))
            blocks[i, layer] = block
        out = [jnp.zeros((g.shape[0], GROUP, *g.shape[1:]), BF) for g in gradients]
        for i, layer in units:
            block = blocks[i, layer]
            of_far = lax.ppermute(block, "dp", far)
            of_near = lax.ppermute(block, "dp", near)
            of_across = lax.ppermute(of_far, "dp", near)
            for which, part in ((me, block), (me ^ 1, of_near), (me ^ 2, of_far), (me ^ 3, of_across)):
                out[i] = lax.dynamic_update_slice(out[i], part[None, None], (layer, which, 0, 0))
        new_w = [o.reshape(w.shape) for o, w in zip(out, weights, strict=True)]
        new_m, new_v = [], []
        for own, m, v, g in zip(mine, ms, vs, gradients, strict=True):
            _, m, v = adamw(own, m, v, g, factor)
            new_m.append(m)
            new_v.append(v)
        return (*new_w, *new_m, *new_v)

    sequences, whole, rows = P(("rep", "dp")), P(), P(None, "dp")
    return jax.shard_map(
        step,
        mesh=mesh,
        in_specs=(sequences, sequences) + (whole,) * 3 + (rows,) * 6,
        out_specs=(P("rep"),) * 3 + (P("rep", "dp"),) * 6,
        check_vma=False,
    )
```

profile of v0, /device:TPU:0, one launch (start us, length us, event | category | flops | bytes accessed | tf_op | source)
XLA Modules:
  0.0 447.2 jit_solution(15043043347842455602)
XLA Ops:
  0.6 53.5 %forward.1 = (f32[5,2048,512]{2,1,0:T(8,128)}, f32[5,2048,512]{2,1,0:T(8,128)}, bf16[5,2048,512]{2,1,0:T(8,128)(2,1)}, bf16[2048,896]{1,0:T(8,128)(2,1)}, bf16[2...) custom-call(bf16[1,2048,896]{2,1,0:T(8,128)(2,1)} %x.1, bf16[2,896,2560]{2,1,0:T(8,128)(2,1)} %wg.3, ...), custom_call_target="tpu_custom_call" | custom-call | flops 28185722880 | bytes 80000000 | tf_op jit(solution)/shard_map/forward/pallas_call | solution.py:92
  54.2 205.5 %backward.1 = (bf16[2,224,2560]{2,1,0:T(8,128)(2,1)}, bf16[2,224,2560]{2,1,0:T(8,128)(2,1)}, bf16[2,640,896]{2,1,0:T(8,128)(2,1)}, f32[8,128]{1,0:T(8,128)}) custom-call(bf16[2048,896]{1,0:T(8,128)(2,1)} %get-tuple-element.32.a1, bf16[896,2048]{1,0:T(8,128)(2,1)} %get-tuple-element.33.a1t, bf16[2048,896]{1,0:T(8,128)(2,1)} %bitcast.167, ...), custom_call_target="tpu_custom_call" | custom-call | flops 112742891520 | bytes 130000000 | tf_op jit(solution)/shard_map/backward/pallas_call | solution.py:321
  259.6 1.2 slice.84
  261.5 0.0 slice-start.6
  261.5 5.3 %fusion.5 = bf16[224,2560]{1,0:T(8,128)(2,1)} fusion(f32[2,224,2560]{2,1,0:T(8,128)} %param.19, f32[2,224,2560]{2,1,0:T(8,128)} %param.16, bf16[2,4,224,2560]{3,2,1,0:T(8,128)(2,1)} %bitcast.161, s32[]{:T(128)S(6)} %select_n.13, f32[]{:T(128)} %bitcast.4, bf16[2,224,2560]{2,1,0:T(8,128)(2,1)} %get-tuple-element.39), kind=kLoop, calls=%fused_computation.32 | loop fusion | flops 9748480 | bytes 8028168 | tf_op jit(solution)/shard_map/convert_element_type | solution.py:367
  266.8 5.4 %fusion.8 = bf16[224,2560]{1,0:T(8,128)(2,1)} fusion(f32[2,224,2560]{2,1,0:T(8,128)} %param.19, f32[2,224,2560]{2,1,0:T(8,128)} %param.16, bf16[2,4,224,2560]{3,2,1,0:T(8,128)(2,1)} %bitcast.162, s32[]{:T(128)S(6)} %add.166, s32[]{:T(128)S(6)} %select_n.13, f32[]{:T(128)} %bitcast.4, bf16[2,224,2560]{2,1,0:T(8,128)(2,1)} %get-tuple-element.39), kind=kLoop, calls=%fused_computation.35 | loop fusion | flops 9748480 | bytes 8028172 | tf_op jit(solution)/shard_map/convert_element_type | solution.py:367
  272.3 5.1 %fusion.11 = bf16[224,2560]{1,0:T(8,128)(2,1)} fusion(f32[2,224,2560]{2,1,0:T(8,128)} %param.20, f32[2,224,2560]{2,1,0:T(8,128)} %param.17, bf16[2,4,224,2560]{3,2,1,0:T(8,128)(2,1)} %bitcast.163, s32[]{:T(128)S(6)} %select_n.13, f32[]{:T(128)} %bitcast.4, bf16[2,224,2560]{2,1,0:T(8,128)(2,1)S(1)} %copy-done.2), kind=kLoop, calls=%fused_computation.38 | loop fusion | flops 9748480 | bytes 8028168 | tf_op jit(solution)/shard_map/convert_element_type | solution.py:367
  277.4 0.0 slice-start.3
  277.4 4.4 fusion.14
  281.9 3.6 fusion.17
  285.5 0.0 collective-permute-start.12
  285.5 2.4 collective-permute-start.13
  287.9 0.1 collective-permute-start.6
  288.0 0.3 collective-permute-start.7
  288.3 0.1 collective-permute-start
  288.4 3.7 fusion.20
  292.1 6.7 %fusion.2 = (f32[2,640,896]{2,1,0:T(8,128)}, f32[2,640,896]{2,1,0:T(8,128)}) fusion(f32[2,640,896]{2,1,0:T(8,128)S(1)} %bitcast.153, bf16[2,640,896]{2,1,0:T(8,128)(2,1)} %get-tuple-element.49, f32[]{:T(128)} %bitcast.4, f32[2,640,896]{2,1,0:T(8,128)S(1)} %bitcast.155), kind=kLoop, calls=%fused_computation.5 | loop fusion | flops 10321920 | bytes 20643844 | tf_op jit(solution)/shard_map/add | solution.py:366
  298.8 13.7 %fusion = (f32[2,224,2560]{2,1,0:T(8,128)}, f32[2,224,2560]{2,1,0:T(8,128)}, f32[2,224,2560]{2,1,0:T(8,128)}, f32[2,224,2560]{2,1,0:T(8,128)}) fusion(f32[2,224,2560]{2,1,0:T(8,128)S(1)} %bitcast.157, bf16[2,224,2560]{2,1,0:T(8,128)(2,1)} %get-tuple-element.39, f32[]{:T(128)} %bitcast.4, f32[2,224,2560]{2,1,0:T(8,128)} %param.16, ...), kind=kLoop, calls=%fused_computation.3 | loop fusion | flops 20643840 | bytes 41287684 | tf_op jit(solution)/shard_map/add | solution.py:366
  312.5 4.4 broadcast.79.clone.1
  316.9 2.3 bitcast_dynamic-update-slice_fusion.15
  319.2 4.4 broadcast.79.clone
  323.7 2.3 bitcast_dynamic-update-slice_fusion.23
  326.0 1.2 broadcast_in_dim.91
  327.2 1.5 bitcast_dynamic-update-slice_fusion.7
  328.7 0.0 collective-permute-done.6
  328.7 0.1 copy-done.4
  328.8 0.4 collective-permute-start.15
  329.2 2.3 bitcast_dynamic-update-slice_fusion.14
  331.5 0.0 collective-permute-done
  331.5 1.7 collective-permute-start.16
  333.3 2.3 bitcast_dynamic-update-slice_fusion.22
  335.6 3.3 collective-permute-done.7
  338.9 2.0 collective-permute-start.1
  340.9 2.3 bitcast_dynamic-update-slice_fusion.13
  343.2 1.4 bitcast_dynamic-update-slice_fusion.6
  344.7 0.0 collective-permute-done.13
  344.7 0.5 collective-permute-start.9
  345.2 1.4 bitcast_dynamic-update-slice_fusion.5
  346.7 41.0 %collective-permute-done.1 = bf16[224,2560]{1,0:T(8,128)(2,1)S(1)} collective-permute-done((bf16[224,2560]{1,0:T(8,128)(2,1)}, bf16[224,2560]{1,0:T(8,128)(2,1)S(1)}, u32[]{:S(2)}, u32[]{:S(2)}) %collective-permute-start.1) | collective-permute-done | bytes 1146912 | tf_op jit(solution)/shard_map/ppermute | solution.py:381
  387.6 1.7 collective-permute-start.10
  389.4 1.1 bitcast_dynamic-update-slice_fusion.21
  390.5 1.1 bitcast_dynamic-update-slice_fusion.12
  391.5 1.1 bitcast_dynamic-update-slice_fusion.11
  392.6 0.6 collective-permute-done.2
  393.3 0.3 collective-permute-start.4
  393.5 1.1 bitcast_dynamic-update-slice_fusion.20
  394.6 1.1 bitcast_dynamic-update-slice_fusion.19
  395.7 1.1 bitcast_dynamic-update-slice_fusion.10
  396.8 19.0 %collective-permute-done.10 = bf16[224,2560]{1,0:T(8,128)(2,1)S(1)} collective-permute-done((bf16[224,2560]{1,0:T(8,128)(2,1)S(1)}, bf16[224,2560]{1,0:T(8,128)(2,1)S(1)}, u32[]{:S(2)}, u32[]{:S(2)}) %collective-permute-start.10) | collective-permute-done | bytes 1146912 | tf_op jit(solution)/shard_map/ppermute | solution.py:381
  415.8 1.1 bitcast_dynamic-update-slice_fusion.9
  416.9 0.5 collective-permute-start.11
  417.4 21.8 %collective-permute-done.4 = bf16[224,2560]{1,0:T(8,128)(2,1)S(1)} collective-permute-done((bf16[224,2560]{1,0:T(8,128)(2,1)S(1)}, bf16[224,2560]{1,0:T(8,128)(2,1)S(1)}, u32[]{:S(2)}, u32[]{:S(2)}) %collective-permute-start.4) | collective-permute-done | bytes 1146912 | tf_op jit(solution)/shard_map/ppermute | solution.py:381
  439.2 0.5 collective-permute-start.5
  439.7 0.2 bitcast_dynamic-update-slice_fusion.4
  439.9 0.2 bitcast_dynamic-update-slice_fusion.3
  440.1 1.1 bitcast_dynamic-update-slice_fusion.18
  441.2 0.2 bitcast_dynamic-update-slice_fusion.2
  441.4 1.1 bitcast_dynamic-update-slice_fusion.17
  442.4 0.2 bitcast_dynamic-update-slice_fusion.1
  442.6 0.2 bitcast_dynamic-update-slice_fusion
  442.8 0.0 copy-start.1
  442.8 1.2 bitcast_dynamic-update-slice_fusion.8
  444.0 1.6 bitcast_dynamic-update-slice_fusion.16
  445.7 1.5 copy-done.1
  (42 shorter events, 0.1 us)
Async XLA Ops:
  261.5 15.9 %slice-start.6 = ((s8[4587520]{0:T(1024)(128)(4,1)}), s8[393216]{0:T(1024)(128)(4,1)S(1)}, s32[]{:S(2)}) async-start(s8[4587520]{0:T(1024)(128)(4,1)} %bitcast.158), calls=%async_computation.6 | async-start | bytes 786432
  266.8 5.5 %copy-start.2 = (bf16[2,224,2560]{2,1,0:T(8,128)(2,1)S(1)}, bf16[2,224,2560]{2,1,0:T(8,128)(2,1)}, u32[]{:S(2)}) copy-start(bf16[2,224,2560]{2,1,0:T(8,128)(2,1)} %get-tuple-element.44) | copy-start | bytes 6881284
  266.8 10.6 %slice-start.7 = ((s8[4587520]{0:T(1024)(128)(4,1)}), s8[4194304]{0:T(1024)(128)(4,1)S(1)}, s32[]{:S(2)}) async-start(s8[4587520]{0:T(1024)(128)(4,1)} %bitcast.158), calls=%async_computation.7 | async-start | bytes 8388608
  272.3 9.5 %slice-start = ((s8[4587520]{0:T(1024)(128)(4,1)}), s8[4194304]{0:T(1024)(128)(4,1)S(1)}, s32[]{:S(2)}) async-start(s8[4587520]{0:T(1024)(128)(4,1)} %bitcast.152), calls=%async_computation | async-start | bytes 8388608
  272.3 9.5 %slice-start.2 = ((s8[4587520]{0:T(1024)(128)(4,1)}), s8[4194304]{0:T(1024)(128)(4,1)S(1)}, s32[]{:S(2)}) async-start(s8[4587520]{0:T(1024)(128)(4,1)} %bitcast.154), calls=%async_computation.2 | async-start | bytes 8388608
  277.4 4.4 slice-start.1
  277.4 4.4 slice-start.3
  277.4 4.4 copy-start
  285.5 57.7 %collective-permute-start.12 = (bf16[640,896]{1,0:T(8,128)(2,1)}, bf16[640,896]{1,0:T(8,128)(2,1)}, u32[]{:S(2)}, u32[]{:S(2)}) collective-permute-start(bf16[640,896]{1,0:T(8,128)(2,1)} %fusion.17), channel_id=1, source_target_pairs={{0,1},{1,0},{2,3},{3,2},{4,5},{5,4},{6,7},{7,6}} | collective-permute-start | bytes 3440648 | tf_op jit(solution)/shard_map/ppermute | solution.py:382
  285.5 59.2 %collective-permute-start.13 = (bf16[640,896]{1,0:T(8,128)(2,1)}, bf16[640,896]{1,0:T(8,128)(2,1)}, u32[]{:S(2)}, u32[]{:S(2)}) collective-permute-start(bf16[640,896]{1,0:T(8,128)(2,1)} %fusion.17), channel_id=1, source_target_pairs={{0,2},{1,3},{2,0},{3,1},{4,6},{5,7},{6,4},{7,5}} | collective-permute-start | bytes 3440648 | tf_op jit(solution)/shard_map/ppermute | solution.py:381
  287.9 40.9 %collective-permute-start.6 = (bf16[224,2560]{1,0:T(8,128)(2,1)}, bf16[224,2560]{1,0:T(8,128)(2,1)}, u32[]{:S(2)}, u32[]{:S(2)}) collective-permute-start(bf16[224,2560]{1,0:T(8,128)(2,1)} %fusion.11), channel_id=1, source_target_pairs={{0,1},{1,0},{2,3},{3,2},{4,5},{5,4},{6,7},{7,6}} | collective-permute-start | bytes 3440648 | tf_op jit(solution)/shard_map/ppermute | solution.py:382
  288.0 50.9 %collective-permute-start.7 = (bf16[224,2560]{1,0:T(8,128)(2,1)}, bf16[224,2560]{1,0:T(8,128)(2,1)}, u32[]{:S(2)}, u32[]{:S(2)}) collective-permute-start(bf16[224,2560]{1,0:T(8,128)(2,1)} %fusion.11), channel_id=1, source_target_pairs={{0,2},{1,3},{2,0},{3,1},{4,6},{5,7},{6,4},{7,5}} | collective-permute-start | bytes 3440648 | tf_op jit(solution)/shard_map/ppermute | solution.py:381
  288.3 43.3 %collective-permute-start = (bf16[224,2560]{1,0:T(8,128)(2,1)}, bf16[224,2560]{1,0:T(8,128)(2,1)}, u32[]{:S(2)}, u32[]{:S(2)}) collective-permute-start(bf16[224,2560]{1,0:T(8,128)(2,1)} %fusion.5), channel_id=1, source_target_pairs={{0,1},{1,0},{2,3},{3,2},{4,5},{5,4},{6,7},{7,6}} | collective-permute-start | bytes 3440648 | tf_op jit(solution)/shard_map/ppermute | solution.py:382
  288.4 10.4 %slice-start.4 = ((s8[4587520]{0:T(1024)(128)(4,1)}), s8[4194304]{0:T(1024)(128)(4,1)S(1)}, s32[]{:S(2)}) async-start(s8[4587520]{0:T(1024)(128)(4,1)} %bitcast.156), calls=%async_computation.4 | async-start | bytes 8388608
  292.1 6.7 %slice-start.5 = ((s8[4587520]{0:T(1024)(128)(4,1)}), s8[393216]{0:T(1024)(128)(4,1)S(1)}, s32[]{:S(2)}) async-start(s8[4587520]{0:T(1024)(128)(4,1)} %bitcast.156), calls=%async_computation.5 | async-start | bytes 786432
  327.2 1.6 copy-start.4
  328.8 112.4 %collective-permute-start.15 = (bf16[640,896]{1,0:T(8,128)(2,1)S(1)}, bf16[640,896]{1,0:T(8,128)(2,1)S(1)}, u32[]{:S(2)}, u32[]{:S(2)}) collective-permute-start(bf16[640,896]{1,0:T(8,128)(2,1)S(1)} %copy-done.4), channel_id=1, source_target_pairs={{0,1},{1,0},{2,3},{3,2},{4,5},{5,4},{6,7},{7,6}} | collective-permute-start | bytes 3440648 | tf_op jit(solution)/shard_map/ppermute | solution.py:382
  331.5 85.3 %collective-permute-start.16 = (bf16[640,896]{1,0:T(8,128)(2,1)S(1)}, bf16[640,896]{1,0:T(8,128)(2,1)S(1)}, u32[]{:S(2)}, u32[]{:S(2)}) collective-permute-start(bf16[640,896]{1,0:T(8,128)(2,1)S(1)} %copy-done.4), channel_id=1, source_target_pairs={{0,2},{1,3},{2,0},{3,1},{4,6},{5,7},{6,4},{7,5}} | collective-permute-start | bytes 3440648 | tf_op jit(solution)/shard_map/ppermute | solution.py:381
  335.6 9.1 %copy-start.5 = (bf16[224,2560]{1,0:T(8,128)(2,1)S(1)}, bf16[224,2560]{1,0:T(8,128)(2,1)}, u32[]{:S(2)}) copy-start(bf16[224,2560]{1,0:T(8,128)(2,1)} %fusion.14) | copy-start | bytes 3440644
  338.9 48.8 %collective-permute-start.1 = (bf16[224,2560]{1,0:T(8,128)(2,1)}, bf16[224,2560]{1,0:T(8,128)(2,1)S(1)}, u32[]{:S(2)}, u32[]{:S(2)}) collective-permute-start(bf16[224,2560]{1,0:T(8,128)(2,1)} %fusion.5), channel_id=1, source_target_pairs={{0,2},{1,3},{2,0},{3,1},{4,6},{5,7},{6,4},{7,5}} | collective-permute-start | bytes 3440648 | tf_op jit(solution)/shard_map/ppermute | solution.py:381
  343.2 47.2 %collective-permute-start.8 = (bf16[224,2560]{1,0:T(8,128)(2,1)}, bf16[224,2560]{1,0:T(8,128)(2,1)S(1)}, u32[]{:S(2)}, u32[]{:S(2)}) collective-permute-start(bf16[224,2560]{1,0:T(8,128)(2,1)} %collective-permute-done.7), channel_id=1, source_target_pairs={{0,1},{1,0},{2,3},{3,2},{4,5},{5,4},{6,7},{7,6}} | collective-permute-start | bytes 3440648 | tf_op jit(solution)/shard_map/ppermute | solution.py:383
  344.7 51.0 %collective-permute-start.9 = (bf16[224,2560]{1,0:T(8,128)(2,1)S(1)}, bf16[224,2560]{1,0:T(8,128)(2,1)S(1)}, u32[]{:S(2)}, u32[]{:S(2)}) collective-permute-start(bf16[224,2560]{1,0:T(8,128)(2,1)S(1)} %copy-done.5), channel_id=1, source_target_pairs={{0,1},{1,0},{2,3},{3,2},{4,5},{5,4},{6,7},{7,6}} | collective-permute-start | bytes 3440648 | tf_op jit(solution)/shard_map/ppermute | solution.py:382
  387.6 28.1 %collective-permute-start.10 = (bf16[224,2560]{1,0:T(8,128)(2,1)S(1)}, bf16[224,2560]{1,0:T(8,128)(2,1)S(1)}, u32[]{:S(2)}, u32[]{:S(2)}) collective-permute-start(bf16[224,2560]{1,0:T(8,128)(2,1)S(1)} %copy-done.5), channel_id=1, source_target_pairs={{0,2},{1,3},{2,0},{3,1},{4,6},{5,7},{6,4},{7,5}} | collective-permute-start | bytes 3440648 | tf_op jit(solution)/shard_map/ppermute | solution.py:381
  390.5 2.8 copy-start.3
  390.5 2.8 collective-permute-start.2
  393.3 45.9 %collective-permute-start.4 = (bf16[224,2560]{1,0:T(8,128)(2,1)S(1)}, bf16[224,2560]{1,0:T(8,128)(2,1)S(1)}, u32[]{:S(2)}, u32[]{:S(2)}) collective-permute-start(bf16[224,2560]{1,0:T(8,128)(2,1)S(1)} %copy-done.3), channel_id=1, source_target_pairs={{0,2},{1,3},{2,0},{3,1},{4,6},{5,7},{6,4},{7,5}} | collective-permute-start | bytes 3440648 | tf_op jit(solution)/shard_map/ppermute | solution.py:381
  395.7 43.5 %collective-permute-start.14 = (bf16[640,896]{1,0:T(8,128)(2,1)}, bf16[640,896]{1,0:T(8,128)(2,1)S(1)}, u32[]{:S(2)}, u32[]{:S(2)}) collective-permute-start(bf16[640,896]{1,0:T(8,128)(2,1)} %collective-permute-done.13), channel_id=1, source_target_pairs={{0,1},{1,0},{2,3},{3,2},{4,5},{5,4},{6,7},{7,6}} | collective-permute-start | bytes 3440648 | tf_op jit(solution)/shard_map/ppermute | solution.py:383
  415.8 24.3 %collective-permute-start.3 = (bf16[224,2560]{1,0:T(8,128)(2,1)S(1)}, bf16[224,2560]{1,0:T(8,128)(2,1)S(1)}, u32[]{:S(2)}, u32[]{:S(2)}) collective-permute-start(bf16[224,2560]{1,0:T(8,128)(2,1)S(1)} %copy-done.3), channel_id=1, source_target_pairs={{0,1},{1,0},{2,3},{3,2},{4,5},{5,4},{6,7},{7,6}} | collective-permute-start | bytes 3440648 | tf_op jit(solution)/shard_map/ppermute | solution.py:382
  416.9 26.0 %collective-permute-start.11 = (bf16[224,2560]{1,0:T(8,128)(2,1)S(1)}, bf16[224,2560]{1,0:T(8,128)(2,1)S(1)}, u32[]{:S(2)}, u32[]{:S(2)}) collective-permute-start(bf16[224,2560]{1,0:T(8,128)(2,1)S(1)} %collective-permute-done.10), channel_id=1, source_target_pairs={{0,1},{1,0},{2,3},{3,2},{4,5},{5,4},{6,7},{7,6}} | collective-permute-start | bytes 3440648 | tf_op jit(solution)/shard_map/ppermute | solution.py:383
  439.2 3.4 collective-permute-start.17
  439.2 4.8 %collective-permute-start.5 = (bf16[224,2560]{1,0:T(8,128)(2,1)S(1)}, bf16[224,2560]{1,0:T(8,128)(2,1)S(1)}, u32[]{:S(2)}, u32[]{:S(2)}) collective-permute-start(bf16[224,2560]{1,0:T(8,128)(2,1)S(1)} %collective-permute-done.4), channel_id=1, source_target_pairs={{0,1},{1,0},{2,3},{3,2},{4,5},{5,4},{6,7},{7,6}} | collective-permute-start | bytes 3440648 | tf_op jit(solution)/shard_map/ppermute | solution.py:383
  442.8 4.3 copy-start.1
where the time goes:
time: 448 us; the launch traced here: 447 us
  Pallas kernels  259 us (58%)
  waiting for transfers between devices  85.7 us (19%)
  other arithmetic  48 us (11%)
  local copies, waits for them, and re-layouts  42.3 us (9%)
  starting transfers between devices  10.6 us (2%)
    pallas_call x1, Pallas kernels, backward(): pl.pallas_call(backward_kernel, out_shape=[jax.ShapeDtypeStruct((2, OWN_D...  205 us
    ppermute x6, waiting for transfers between devices, step(): of_far = lax.ppermute(block, 'dp', far)  85.1 us
    pallas_call x1, Pallas kernels, forward(): pl.pallas_call(forward_kernel, grid=(TILES,), out_shape=[wide, wide, jax....  53.5 us
    dynamic_update_slice x24, local copies, waits for them, and re-layouts, step(): lax.dynamic_update_slice(out[i], part[None, None], (layer, which, 0, 0))  29.5 us
    convert_element_type x6, other arithmetic, adamw(): (w.astype(F32) - 0.02 * (m * lax.rsqrt(v + 1e-08) + 0.1 * w.astype(F32)))...  27.6 us
    add x2, other arithmetic, adamw(): v = 0.95 * v + 0.05 * g * g  20.3 us
  transfers between devices with their start and end apart: 18, of which 5 were waited for; matrix products, arithmetic and copies ran while one was open for 14% of the time, Pallas kernels for 0%

commit v1 on v0

v1 whole, which is shorter than its diff:
```python
import jax
import jax.numpy as jnp
from jax import lax
from jax.experimental import pallas as pl
from jax.experimental.pallas import tpu as pltpu
from jax.sharding import PartitionSpec as P


T, D, FF = 2048, 896, 2560
GROUP = 4
OWN_D, OWN_F = D // GROUP, FF // GROUP
CHUNKS, PIECE = 5, 128
C = GROUP * PIECE
SENDS = 3
OWNS = 3
TILE = 512
TILES = T // TILE
BF, F32 = jnp.bfloat16, jnp.float32
ANY = pl.BlockSpec(memory_space=pl.ANY)


def dot(a, b, over=(1, 0)):
    return lax.dot_general(a, b, (((over[0],), (over[1],)), ((), ())), preferred_element_type=F32)


def logistic(x):
    return 1.0 / (1.0 + jnp.exp(-x))


def normed(h):
    wide = h.astype(F32)
    return (wide * lax.rsqrt(jnp.mean(wide * wide, -1, keepdims=True) + 1e-6)).astype(BF)


def at(i, size):
    return pl.ds(pl.multiple_of(i * size, size), size)


def hidden(d, k):
    return pl.ds(pl.multiple_of(d * OWN_F + k * PIECE, PIECE), PIECE)


def step_kernel(
    x, dy, wg, wu, wd,
    gg, gu, gd, ss, s0, q0, p0, a0t,
    a, atr, dh, h, pr, dg, du, da, sq, wgv, wuv, wdv, dwg, dwd, rdg, rdd, isg, isd, irg, ird, owng, ownd, ssg, ssd, nsend, nrecv,
    isem, wsem, psem, ssem, d2d_send, d2d_recv, ici_send, ici_recv, osem, n_send, n_recv,
):
    me = lax.axis_index("dp")
    core, chip = me % 2, me // 2
    other = 1 - chip
    near, far, across = me + 1 - 2 * core, (me + 2) % 4, 3 - me

    def remote(src, dst, send, recv, to):
        return pltpu.make_async_remote_copy(src, dst, send, recv, device_id={"dp": to}, device_id_type=pl.DeviceIdType.MESH)

    def start(copies):
        for c in copies:
            c.start()

    def wait(copies):
        for c in copies:
            c.wait()

    def weights(layer, k, slot, all_three):
        if all_three:
            for d in range(GROUP):
                yield pltpu.make_async_copy(wg.at[layer, :, hidden(d, k)], wgv.at[slot, :, at(d, PIECE)], wsem.at[slot, 4 + d])
                yield pltpu.make_async_copy(wu.at[layer, :, hidden(d, k)], wuv.at[slot, :, at(d, PIECE)], wsem.at[slot, 8 + d])
        for d in range(GROUP):
            yield pltpu.make_async_copy(wd.at[layer, hidden(d, k), :], wdv.at[slot, at(d, PIECE), :], wsem.at[slot, d])

    def product_out(k):
        return pltpu.make_async_copy(pr.at[k % 2], p0.at[k], psem.at[k % 2])

    def product_in(k):
        return pltpu.make_async_copy(p0.at[k], pr.at[(k + 1) % 2], psem.at[(k + 1) % 2])

    def factors_out(step):
        k, t, slot = step // TILES, step % TILES, step % 2
        return [pltpu.make_async_copy(sq.at[slot, i], f.at[k, at(t, TILE), :], ssem.at[slot, i]) for i, f in enumerate((s0, q0))]

    def silu_in(k, t):
        return pltpu.make_async_copy(s0.at[k, at(t, TILE), :], da.at[at(t, TILE), pl.ds(0, C)], ssem.at[0, t])

    def factor_in(k, t):
        return pltpu.make_async_copy(q0.at[k, at(t, TILE), :], sq.at[t // 2, t % 2], ssem.at[1, t])

    first = [pltpu.make_async_copy(src.at[0], dst, isem.at[i]) for i, (src, dst) in enumerate(((x, h), (dy, dh)))]
    start(first)
    start(weights(0, 0, 0, True))
    barrier = pltpu.get_barrier_semaphore()
    for to in (near, far, across):
        pl.semaphore_signal(barrier, inc=1, device_id={"dp": to}, device_id_type=pl.DeviceIdType.MESH)
    ssg[...] = jnp.zeros_like(ssg)
    ssd[...] = jnp.zeros_like(ssd)
    first[0].wait()

    @pl.loop(0, T // 256)
    def _(t):
        r = at(t, 256)
        n = normed(h[r, :])
        a[r, :] = n
        atr[:, r] = n.T
        da[r, :] = jnp.zeros((256, D), F32)

    turned = pltpu.make_async_copy(atr, a0t, isem.at[2])
    turned.start()


    @pl.loop(0, CHUNKS)
    def _(k):
        slot = k % 2
        wait(weights(0, k, slot, True))

        @pl.when(k < CHUNKS - 1)
        def _():
            start(weights(0, k + 1, 1 - slot, True))

        @pl.when(k == CHUNKS - 1)
        def _():
            start(weights(1, 0, 1 - slot, True))

        @pl.when(k >= 2)
        def _():
            product_out(k - 2).wait()

        @pl.loop(0, TILES)
        def _(t):
            r = at(t, TILE)
            step = k * TILES + t
            gate = dot(a[r, :], wgv[slot])
            up = dot(a[r, :], wuv[slot])
            s = logistic(gate)
            silu = gate * s
            prod = (silu * up).astype(BF)
            pr[slot, r, :] = prod
            da[r, :] += dot(prod, wdv[slot])

            @pl.when(step >= 2)
            def _():
                wait(factors_out(step - 2))

            sq[step % 2, 0] = silu
            sq[step % 2, 1] = up * (s * (1.0 + gate * (1.0 - s)))
            start(factors_out(step))

        product_out(k).start()

    first[1].wait()
    turned.wait()

    @pl.loop(0, T // 256)
    def _(t):
        r = at(t, 256)
        out = (h[r, :].astype(F32) + da[r, :].astype(BF).astype(F32)).astype(BF)
        h[r, :] = out
        n = normed(out)
        a[r, :] = n
        atr[:, r] = n.T
        da[r, :] = jnp.zeros((256, D), F32)

    for last in (2, 1):
        product_out(CHUNKS - last).wait()
        wait(factors_out(CHUNKS * TILES - last))
    pl.semaphore_wait(barrier, 3)
    product_in(0).start()

    def to_near(n, part):
        own, got = ((dwd, rdd), (dwg, rdg))[part]
        return remote(own.at[0], got.at[n % 2], d2d_send.at[part, n], d2d_recv.at[part, n], near)

    def to_far(n, part):
        own, got = ((isd, ird), (isg, irg))[part]
        return remote(own.at[n % SENDS], got.at[n], ici_send.at[part, n], ici_recv.at[part, n], far)

    def gradient_down(slot):
        @pl.loop(0, 2, unroll=True)
        def _(half):
            out = dot(pr[slot, :, at(half, 2 * PIECE)], dh[...], (0, 0)).astype(BF)
            dwd[1 - core, half] = out[:PIECE]
            dwd[core, half] = out[PIECE:]

    def gradient(d, i):
        @pl.loop(0, 2, unroll=True)
        def _(half):
            out = dot(atr[at(half, 2 * OWN_D), :], d[...]).astype(BF)
            rows = slice(i * OWN_D, (i + 1) * OWN_D)
            dwg[1 - core, half, rows, :] = out[:OWN_D]
            dwg[core, half, rows, :] = out[OWN_D:]

    def sum_on_chip(n, part):
        slot, place = n % 2, n % OWNS
        own, got, out, kept = ((dwd, rdd, isd, ownd), (dwg, rdg, isg, owng))[part]
        to_near(n, part).wait()

        @pl.when(n >= SENDS)
        def _():
            to_far(n - SENDS, part).wait_send()

        out[n % SENDS] = (own[1, other].astype(F32) + got[slot, other].astype(F32)).astype(BF)
        to_far(n, part).start()
        kept[place] = own[1, chip].astype(F32) + got[slot, chip].astype(F32)

    def gradients(n, slot):
        gradient_down(slot)
        to_near(n, 0).start()
        gradient(dg, 0)
        sum_on_chip(n, 0)
        gradient(du, 1)
        to_near(n, 1).start()

    def results(n):
        layer, k = 1 - n // CHUNKS, n % CHUNKS
        yield pltpu.make_async_copy(ird.at[n], gd.at[layer, at(k, PIECE), :], osem.at[n, 0])
        for i, out in enumerate((gg, gu)):
            for d in range(GROUP):
                yield pltpu.make_async_copy(
                    irg.at[n, pl.ds(i * OWN_D, OWN_D), at(d, PIECE)], out.at[layer, :, hidden(d, k)], osem.at[n, 1 + i * GROUP + d]
                )

    def finish(n):
        place = n % OWNS
        for part, (own, got, total) in enumerate(((ownd, ird, ssd), (owng, irg, ssg))):
            to_far(n, part).wait_recv()
            g = (own[place] + got[n].astype(F32)).astype(BF)
            got[n] = g
            g = g.astype(F32)
            total[...] += jnp.sum((g * g).reshape(-1, 8, g.shape[-1]), 0)
        start(results(n))


    @pl.loop(0, CHUNKS)
    def _(k):
        slot = (CHUNKS + k) % 2
        wait(weights(1, k, slot, True))

        @pl.when(k < CHUNKS - 1)
        def _():
            start(weights(1, k + 1, 1 - slot, True))

        @pl.when(k == CHUNKS - 1)
        def _():
            start(weights(0, 0, 1 - slot, False))

        @pl.loop(0, TILES)
        def _(t):
            r = at(t, TILE)
            n = a[r, :]
            gate = dot(n, wgv[slot])
            up = dot(n, wuv[slot])
            dp = dot(dh[r, :], wdv[slot], (1, 1)).astype(BF).astype(F32)
            s = logistic(gate)
            silu = gate * s
            pr[0, r, :] = (silu * up).astype(BF)
            dg[r, :] = (dp * (up * (s * (1.0 + gate * (1.0 - s))))).astype(BF)
            du[r, :] = (dp * silu).astype(BF)

        @pl.when(k >= OWNS)
        def _():
            finish(k - OWNS)

        gradients(k, 0)

        @pl.loop(0, TILES)
        def _(t):
            r = at(t, TILE)
            da[r, :] += dot(dg[r, :], wgv[slot], (1, 1)) + dot(du[r, :], wuv[slot], (1, 1))

        sum_on_chip(k, 1)

    start(factor_in(0, t) for t in range(TILES))
    turned = pltpu.make_async_copy(a0t, atr, isem.at[2])
    turned.start()

    @pl.loop(0, T // 256)
    def _(t):
        r = at(t, 256)
        wide = h[r, :].astype(F32)
        scale = lax.rsqrt(jnp.mean(wide * wide, -1, keepdims=True) + 1e-6)
        ct = da[r, :].astype(BF).astype(F32)
        back = scale * ct - wide * (scale * scale * scale * jnp.mean(wide * ct, -1, keepdims=True))
        dh[r, :] = (dh[r, :].astype(F32) + back.astype(BF).astype(F32)).astype(BF)

    start(silu_in(0, t) for t in range(TILES))
    turned.wait()


    @pl.loop(0, CHUNKS)
    def _(k):
        n = CHUNKS + k
        slot = k % 2
        wait(weights(0, k, slot, False))
        product_in(k).wait()

        @pl.when(k < CHUNKS - 1)
        def _():
            start(weights(0, k + 1, 1 - slot, False))
            product_in(k + 1).start()

        @pl.loop(0, TILES)
        def _(t):
            r = at(t, TILE)
            silu_in(k, t).wait()
            factor_in(k, t).wait()
            dp = dot(dh[r, :], wdv[slot], (1, 1)).astype(BF).astype(F32)
            du[r, :] = (dp * da[r, pl.ds(0, C)]).astype(BF)
            dg[r, :] = (dp * sq[t // 2, t % 2]).astype(BF)

        @pl.when(k < CHUNKS - 1)
        def _():
            @pl.loop(0, TILES)
            def _(t):
                silu_in(k + 1, t).start()
                factor_in(k + 1, t).start()

        finish(n - OWNS)
        gradients(n, (k + 1) % 2)
        sum_on_chip(n, 1)

    @pl.loop(2 * CHUNKS - OWNS, 2 * CHUNKS)
    def _(n):
        finish(n)

    for last in range(SENDS):
        for part in range(2):
            to_far(2 * CHUNKS - SENDS + last, part).wait_send()

    nsend[...] = jnp.full((8, 128), jnp.sum(ssg[...]) + jnp.sum(ssd[...]), F32)
    norms = [remote(nsend, nrecv.at[i], n_send.at[i], n_recv.at[i], to) for i, to in enumerate((near, far, across))]
    start(norms)

    @pl.loop(0, 2 * CHUNKS)
    def _(n):
        wait(results(n))

    wait(norms)
    ss[...] = nsend[...] + nrecv[0] + nrecv[1] + nrecv[2]


def gradients_of(*args):
    vmem, sem = pltpu.VMEM, pltpu.SemaphoreType.DMA
    g_rows = 2 * OWN_D
    return pl.pallas_call(
        step_kernel,
        out_shape=[
            jax.ShapeDtypeStruct((2, OWN_D, FF), BF),
            jax.ShapeDtypeStruct((2, OWN_D, FF), BF),
            jax.ShapeDtypeStruct((2, OWN_F, D), BF),
            jax.ShapeDtypeStruct((8, 128), F32),
            jax.ShapeDtypeStruct((CHUNKS, T, C), F32),
            jax.ShapeDtypeStruct((CHUNKS, T, C), F32),
            jax.ShapeDtypeStruct((CHUNKS, T, C), BF),
            jax.ShapeDtypeStruct((D, T), BF),
        ],
        in_specs=[ANY] * 5,
        out_specs=[ANY] * 3 + [pl.BlockSpec(memory_space=pltpu.VMEM)] + [ANY] * 4,
        scratch_shapes=[
            vmem((T, D), BF), vmem((D, T), BF), vmem((T, D), BF), vmem((T, D), BF),
            vmem((2, T, C), BF), vmem((T, C), BF), vmem((T, C), BF), vmem((T, D), F32), vmem((2, 2, TILE, C), F32),
            vmem((2, D, C), BF), vmem((2, D, C), BF), vmem((2, C, D), BF),
            vmem((2, 2, g_rows, C), BF), vmem((2, 2, PIECE, D), BF),
            vmem((2, 2, g_rows, C), BF), vmem((2, 2, PIECE, D), BF),
            vmem((SENDS, g_rows, C), BF), vmem((SENDS, PIECE, D), BF),
            vmem((2 * CHUNKS, g_rows, C), BF), vmem((2 * CHUNKS, PIECE, D), BF),
            vmem((OWNS, g_rows, C), F32), vmem((OWNS, PIECE, D), F32),
            vmem((8, C), F32), vmem((8, D), F32), vmem((8, 128), F32), vmem((3, 8, 128), F32),
            sem((3,)), sem((2, 12)), sem((2,)), sem((2, TILES)),
            sem((2, 2 * CHUNKS)), sem((2, 2 * CHUNKS)), sem((2, 2 * CHUNKS)), sem((2, 2 * CHUNKS)),
            sem((2 * CHUNKS, 9)), sem((3,)), sem((3,)),
        ],
        compiler_params=pltpu.CompilerParams(vmem_limit_bytes=67_000_000, collective_id=0, has_side_effects=True),
        cost_estimate=pl.CostEstimate(flops=30 * T * D * FF, bytes_accessed=200_000_000, transcendentals=2 * T * FF),
        name="gradients",
    )(*args)[:4]


def solution(mesh):
    far = [(d, d ^ 2) for d in range(GROUP)]
    near = [(d, d ^ 1) for d in range(GROUP)]

    def step(x, dy, *arrays):
        weights, ms, vs = (arrays[i : i + 3] for i in (0, 3, 6))
        me = lax.axis_index("dp")
        *gradients, squares = gradients_of(x, dy, *weights)
        count = sum(w.size for w in weights)
        factor = jnp.minimum(1.0, 0.5 * lax.rsqrt(squares[0, 0] / count + 1e-30))

        def adamw(w, m, v, g, factor):
            g = g.astype(F32) * factor
            m = 0.9 * m + 0.1 * g
            v = 0.95 * v + 0.05 * g * g
            return (w.astype(F32) - 0.02 * (m * lax.rsqrt(v + 1e-8) + 0.1 * w.astype(F32))).astype(BF), m, v

        mine = []
        for w, g in zip(weights, gradients, strict=True):
            mine.append(lax.dynamic_index_in_dim(w.reshape(g.shape[0], GROUP, *g.shape[1:]), me, 1, keepdims=False))
        units = [(i, layer) for i in range(3) for layer in range(2)]
        blocks = {}
        for i, layer in units:
            block = adamw(mine[i][layer], ms[i][layer], vs[i][layer], gradients[i][layer], factor)[0]
            block, factor = lax.optimization_barrier((block, factor))
            blocks[i, layer] = block
        out = [jnp.zeros((g.shape[0], GROUP, *g.shape[1:]), BF) for g in gradients]
        for i, layer in units:
            block = blocks[i, layer]
            of_far = lax.ppermute(block, "dp", far)
            of_near = lax.ppermute(block, "dp", near)
            of_across = lax.ppermute(of_far, "dp", near)
            for which, part in ((me, block), (me ^ 1, of_near), (me ^ 2, of_far), (me ^ 3, of_across)):
                out[i] = lax.dynamic_update_slice(out[i], part[None, None], (layer, which, 0, 0))
        new_w = [o.reshape(w.shape) for o, w in zip(out, weights, strict=True)]
        new_m, new_v = [], []
        for own, m, v, g in zip(mine, ms, vs, gradients, strict=True):
            _, m, v = adamw(own, m, v, g, factor)
            new_m.append(m)
            new_v.append(v)
        return (*new_w, *new_m, *new_v)

    sequences, whole, rows = P(("rep", "dp")), P(), P(None, "dp")
    return jax.shard_map(
        step,
        mesh=mesh,
        in_specs=(sequences, sequences) + (whole,) * 3 + (rows,) * 6,
        out_specs=(P("rep"),) * 3 + (P("rep", "dp"),) * 6,
        check_vma=False,
    )
```

time: 448 us -> 437 us (0.975)
  Pallas kernels: 259 us -> 249 us
    pallas_call x2 -> x1, Pallas kernels: 259 us -> 249 us  [gradients_of(): pl.pallas_call(step_kernel, out_shape=[jax.ShapeDtypeStruct((2, OWN_D, FF...]
where the time goes in v1:
time: 437 us
  Pallas kernels  249 us (57%)
  waiting for transfers between devices  85.7 us (20%)
  other arithmetic  47.1 us (11%)
  local copies, waits for them, and re-layouts  42.3 us (10%)
  starting transfers between devices  10.6 us (2%)
    pallas_call x1, Pallas kernels, gradients_of(): pl.pallas_call(step_kernel, out_shape=[jax.ShapeDtypeStruct((2, OWN_D, FF...  249 us
    ppermute x6, waiting for transfers between devices, step(): of_far = lax.ppermute(block, 'dp', far)  85.1 us
    dynamic_update_slice x24, local copies, waits for them, and re-layouts, step(): lax.dynamic_update_slice(out[i], part[None, None], (layer, which, 0, 0))  29.4 us
    convert_element_type x6, other arithmetic, adamw(): (w.astype(F32) - 0.02 * (m * lax.rsqrt(v + 1e-08) + 0.1 * w.astype(F32)))...  26.7 us
    add x2, other arithmetic, adamw(): v = 0.95 * v + 0.05 * g * g  20.3 us
    another operation x2, local copies, waits for them, and re-layouts  8.87 us
  transfers between devices with their start and end apart: 18, of which 5 were waited for; matrix products, arithmetic and copies ran while one was open for 14% of the time, Pallas kernels for 0%

profile of v1, /device:TPU:0, one launch (start us, length us, event | category | flops | bytes accessed | tf_op | source)
XLA Modules:
  0.0 436.6 jit_solution(885300649852908488)
XLA Ops:
  0.6 249.3 %gradients.1 = (bf16[2,224,2560]{2,1,0:T(8,128)(2,1)}, bf16[2,224,2560]{2,1,0:T(8,128)(2,1)}, bf16[2,640,896]{2,1,0:T(8,128)(2,1)}, f32[8,128]{1,0:T(8,128)}, f3...) custom-call(bf16[1,2048,896]{2,1,0:T(8,128)(2,1)} %x.1, ...), custom_call_target="tpu_custom_call" | custom-call | flops 140928614400 | bytes 200000000 | tf_op jit(solution)/shard_map/gradients/pallas_call | solution.py:344
  249.9 1.2 slice.84
  251.8 0.0 slice-start.6
  251.8 5.3 %fusion.5 = bf16[224,2560]{1,0:T(8,128)(2,1)} fusion(f32[2,224,2560]{2,1,0:T(8,128)} %param.19, f32[2,224,2560]{2,1,0:T(8,128)} %param.16, bf16[2,4,224,2560]{3,2,1,0:T(8,128)(2,1)} %bitcast.160, s32[]{:T(128)S(6)} %select_n.13, f32[]{:T(128)} %bitcast.3, bf16[2,224,2560]{2,1,0:T(8,128)(2,1)} %get-tuple-element.25), kind=kLoop, calls=%fused_computation.32 | loop fusion | flops 9748480 | bytes 8028168 | tf_op jit(solution)/shard_map/convert_element_type | solution.py:393
  257.2 5.5 %fusion.8 = bf16[224,2560]{1,0:T(8,128)(2,1)} fusion(f32[2,224,2560]{2,1,0:T(8,128)} %param.19, f32[2,224,2560]{2,1,0:T(8,128)} %param.16, bf16[2,4,224,2560]{3,2,1,0:T(8,128)(2,1)} %bitcast.161, s32[]{:T(128)S(6)} %add.166, s32[]{:T(128)S(6)} %select_n.13, f32[]{:T(128)} %bitcast.3, bf16[2,224,2560]{2,1,0:T(8,128)(2,1)} %get-tuple-element.25), kind=kLoop, calls=%fused_computation.35 | loop fusion | flops 9748480 | bytes 8028172 | tf_op jit(solution)/shard_map/convert_element_type | solution.py:393
  262.6 4.9 %fusion.11 = bf16[224,2560]{1,0:T(8,128)(2,1)} fusion(f32[2,224,2560]{2,1,0:T(8,128)S(1)} %copy-done, f32[2,224,2560]{2,1,0:T(8,128)} %param.17, bf16[2,4,224,2560]{3,2,1,0:T(8,128)(2,1)} %bitcast.162, s32[]{:T(128)S(6)} %select_n.13, f32[]{:T(128)} %bitcast.3, bf16[2,224,2560]{2,1,0:T(8,128)(2,1)} %get-tuple-element.30), kind=kLoop, calls=%fused_computation.38 | loop fusion | flops 9748480 | bytes 8028168 | tf_op jit(solution)/shard_map/convert_element_type | solution.py:393
  267.5 0.0 slice-start.1
  267.5 0.0 slice-start.3
  267.6 3.7 fusion.14
  271.3 3.6 fusion.17
  275.0 0.0 collective-permute-start.12
  275.0 2.4 collective-permute-start.13
  277.3 0.1 collective-permute-start.6
  277.4 0.3 collective-permute-start.7
  277.7 0.1 collective-permute-start
  277.8 3.7 fusion.20
  281.6 6.7 %fusion.2 = (f32[2,640,896]{2,1,0:T(8,128)}, f32[2,640,896]{2,1,0:T(8,128)}) fusion(f32[2,640,896]{2,1,0:T(8,128)S(1)} %bitcast.152, bf16[2,640,896]{2,1,0:T(8,128)(2,1)} %get-tuple-element.35, f32[]{:T(128)} %bitcast.3, f32[2,640,896]{2,1,0:T(8,128)S(1)} %bitcast.154), kind=kLoop, calls=%fused_computation.5 | loop fusion | flops 10321920 | bytes 20643844 | tf_op jit(solution)/shard_map/add | solution.py:392
  288.2 13.7 %fusion = (f32[2,224,2560]{2,1,0:T(8,128)}, f32[2,224,2560]{2,1,0:T(8,128)}, f32[2,224,2560]{2,1,0:T(8,128)}, f32[2,224,2560]{2,1,0:T(8,128)}) fusion(f32[2,224,2560]{2,1,0:T(8,128)S(1)} %bitcast.156, bf16[2,224,2560]{2,1,0:T(8,128)(2,1)} %get-tuple-element.25, f32[]{:T(128)} %bitcast.3, f32[2,224,2560]{2,1,0:T(8,128)} %param.16, ...), kind=kLoop, calls=%fused_computation.3 | loop fusion | flops 20643840 | bytes 41287684 | tf_op jit(solution)/shard_map/add | solution.py:392
  301.9 4.4 %broadcast.79.clone.1 = bf16[2,4,224,2560]{3,2,1,0:T(8,128)(2,1)} broadcast(bf16[]{:T(256)} %constant.17.clone.1), dimensions={} | broadcast | bytes 9175042 | tf_op jit(solution)/shard_map/broadcast.21
  306.3 2.3 bitcast_dynamic-update-slice_fusion.15
  308.7 4.4 %broadcast.79.clone = bf16[2,4,224,2560]{3,2,1,0:T(8,128)(2,1)} broadcast(bf16[]{:T(256)} %constant.17.clone.1), dimensions={} | broadcast | bytes 9175042 | tf_op jit(solution)/shard_map/broadcast.21
  313.1 2.3 bitcast_dynamic-update-slice_fusion.23
  315.4 1.2 broadcast_in_dim.91
  316.6 1.5 bitcast_dynamic-update-slice_fusion.7
  318.2 0.0 collective-permute-done.6
  318.2 0.1 copy-done.5
  318.2 0.4 collective-permute-start.15
  318.6 2.3 bitcast_dynamic-update-slice_fusion.14
  321.0 1.7 collective-permute-start.16
  322.7 2.3 bitcast_dynamic-update-slice_fusion.22
  325.0 3.3 collective-permute-done.7
  328.3 2.0 collective-permute-start.1
  330.3 2.3 bitcast_dynamic-update-slice_fusion.13
  332.7 1.4 bitcast_dynamic-update-slice_fusion.6
  334.1 0.0 collective-permute-done.13
  334.1 0.5 collective-permute-start.9
  334.7 1.4 bitcast_dynamic-update-slice_fusion.5
  336.1 41.0 %collective-permute-done.1 = bf16[224,2560]{1,0:T(8,128)(2,1)S(1)} collective-permute-done((bf16[224,2560]{1,0:T(8,128)(2,1)}, bf16[224,2560]{1,0:T(8,128)(2,1)S(1)}, u32[]{:S(2)}, u32[]{:S(2)}) %collective-permute-start.1) | collective-permute-done | bytes 1146912 | tf_op jit(solution)/shard_map/ppermute | solution.py:407
  377.1 1.7 collective-permute-start.10
  378.8 1.1 bitcast_dynamic-update-slice_fusion.21
  379.9 0.0 collective-permute-done.8
  379.9 1.1 bitcast_dynamic-update-slice_fusion.12
  381.0 1.1 bitcast_dynamic-update-slice_fusion.11
  382.1 0.6 collective-permute-done.2
  382.7 0.3 collective-permute-start.4
  383.0 1.1 bitcast_dynamic-update-slice_fusion.20
  384.1 1.1 bitcast_dynamic-update-slice_fusion.19
  385.1 1.1 bitcast_dynamic-update-slice_fusion.10
  386.2 19.0 %collective-permute-done.10 = bf16[224,2560]{1,0:T(8,128)(2,1)S(1)} collective-permute-done((bf16[224,2560]{1,0:T(8,128)(2,1)S(1)}, bf16[224,2560]{1,0:T(8,128)(2,1)S(1)}, u32[]{:S(2)}, u32[]{:S(2)}) %collective-permute-start.10) | collective-permute-done | bytes 1146912 | tf_op jit(solution)/shard_map/ppermute | solution.py:407
  405.2 1.1 bitcast_dynamic-update-slice_fusion.9
  406.3 0.5 collective-permute-start.11
  406.8 21.8 %collective-permute-done.4 = bf16[224,2560]{1,0:T(8,128)(2,1)S(1)} collective-permute-done((bf16[224,2560]{1,0:T(8,128)(2,1)S(1)}, bf16[224,2560]{1,0:T(8,128)(2,1)S(1)}, u32[]{:S(2)}, u32[]{:S(2)}) %collective-permute-start.4) | collective-permute-done | bytes 1146912 | tf_op jit(solution)/shard_map/ppermute | solution.py:407
  428.7 0.5 collective-permute-start.5
  429.2 0.2 bitcast_dynamic-update-slice_fusion.4
  429.3 0.2 bitcast_dynamic-update-slice_fusion.3
  429.5 1.1 bitcast_dynamic-update-slice_fusion.18
  430.6 0.2 bitcast_dynamic-update-slice_fusion.2
  430.8 1.1 bitcast_dynamic-update-slice_fusion.17
  431.9 0.2 bitcast_dynamic-update-slice_fusion.1
  432.1 0.2 bitcast_dynamic-update-slice_fusion
  432.3 0.0 copy-start.2
  432.3 1.2 bitcast_dynamic-update-slice_fusion.8
  433.4 1.6 bitcast_dynamic-update-slice_fusion.16
  435.1 1.6 copy-done.2
  (43 shorter events, 0.1 us)
Async XLA Ops:
  251.8 15.7 %slice-start.6 = ((s8[4587520]{0:T(1024)(128)(4,1)}), s8[393216]{0:T(1024)(128)(4,1)S(1)}, s32[]{:S(2)}) async-start(s8[4587520]{0:T(1024)(128)(4,1)} %bitcast.157), calls=%async_computation.6 | async-start | bytes 786432
  257.1 5.5 %copy-start = (f32[2,224,2560]{2,1,0:T(8,128)S(1)}, f32[2,224,2560]{2,1,0:T(8,128)}, u32[]{:S(2)}) copy-start(f32[2,224,2560]{2,1,0:T(8,128)} %param.20) | copy-start | bytes 13762564
  257.2 10.4 %slice-start.7 = ((s8[4587520]{0:T(1024)(128)(4,1)}), s8[4194304]{0:T(1024)(128)(4,1)S(1)}, s32[]{:S(2)}) async-start(s8[4587520]{0:T(1024)(128)(4,1)} %bitcast.157), calls=%async_computation.7 | async-start | bytes 8388608
  257.2 10.4 %copy-start.3 = (bf16[2,224,2560]{2,1,0:T(8,128)(2,1)S(1)}, bf16[2,224,2560]{2,1,0:T(8,128)(2,1)}, u32[]{:S(2)}) copy-start(bf16[2,224,2560]{2,1,0:T(8,128)(2,1)} %get-tuple-element.30) | copy-start | bytes 6881284
  262.6 8.7 %slice-start = ((s8[4587520]{0:T(1024)(128)(4,1)}), s8[4194304]{0:T(1024)(128)(4,1)S(1)}, s32[]{:S(2)}) async-start(s8[4587520]{0:T(1024)(128)(4,1)} %bitcast.151), calls=%async_computation | async-start | bytes 8388608
  262.6 8.7 %slice-start.2 = ((s8[4587520]{0:T(1024)(128)(4,1)}), s8[4194304]{0:T(1024)(128)(4,1)S(1)}, s32[]{:S(2)}) async-start(s8[4587520]{0:T(1024)(128)(4,1)} %bitcast.153), calls=%async_computation.2 | async-start | bytes 8388608
  267.5 3.8 slice-start.1
  267.5 3.8 slice-start.3
  267.6 3.7 copy-start.1
  275.0 57.7 %collective-permute-start.12 = (bf16[640,896]{1,0:T(8,128)(2,1)}, bf16[640,896]{1,0:T(8,128)(2,1)}, u32[]{:S(2)}, u32[]{:S(2)}) collective-permute-start(bf16[640,896]{1,0:T(8,128)(2,1)} %fusion.17), channel_id=1, source_target_pairs={{0,1},{1,0},{2,3},{3,2},{4,5},{5,4},{6,7},{7,6}} | collective-permute-start | bytes 3440648 | tf_op jit(solution)/shard_map/ppermute | solution.py:408
  275.0 59.2 %collective-permute-start.13 = (bf16[640,896]{1,0:T(8,128)(2,1)}, bf16[640,896]{1,0:T(8,128)(2,1)}, u32[]{:S(2)}, u32[]{:S(2)}) collective-permute-start(bf16[640,896]{1,0:T(8,128)(2,1)} %fusion.17), channel_id=1, source_target_pairs={{0,2},{1,3},{2,0},{3,1},{4,6},{5,7},{6,4},{7,5}} | collective-permute-start | bytes 3440648 | tf_op jit(solution)/shard_map/ppermute | solution.py:407
  277.3 40.9 %collective-permute-start.6 = (bf16[224,2560]{1,0:T(8,128)(2,1)}, bf16[224,2560]{1,0:T(8,128)(2,1)}, u32[]{:S(2)}, u32[]{:S(2)}) collective-permute-start(bf16[224,2560]{1,0:T(8,128)(2,1)} %fusion.11), channel_id=1, source_target_pairs={{0,1},{1,0},{2,3},{3,2},{4,5},{5,4},{6,7},{7,6}} | collective-permute-start | bytes 3440648 | tf_op jit(solution)/shard_map/ppermute | solution.py:408
  277.4 50.9 %collective-permute-start.7 = (bf16[224,2560]{1,0:T(8,128)(2,1)}, bf16[224,2560]{1,0:T(8,128)(2,1)}, u32[]{:S(2)}, u32[]{:S(2)}) collective-permute-start(bf16[224,2560]{1,0:T(8,128)(2,1)} %fusion.11), channel_id=1, source_target_pairs={{0,2},{1,3},{2,0},{3,1},{4,6},{5,7},{6,4},{7,5}} | collective-permute-start | bytes 3440648 | tf_op jit(solution)/shard_map/ppermute | solution.py:407
  277.7 43.3 %collective-permute-start = (bf16[224,2560]{1,0:T(8,128)(2,1)}, bf16[224,2560]{1,0:T(8,128)(2,1)}, u32[]{:S(2)}, u32[]{:S(2)}) collective-permute-start(bf16[224,2560]{1,0:T(8,128)(2,1)} %fusion.5), channel_id=1, source_target_pairs={{0,1},{1,0},{2,3},{3,2},{4,5},{5,4},{6,7},{7,6}} | collective-permute-start | bytes 3440648 | tf_op jit(solution)/shard_map/ppermute | solution.py:408
  277.8 10.4 %slice-start.4 = ((s8[4587520]{0:T(1024)(128)(4,1)}), s8[4194304]{0:T(1024)(128)(4,1)S(1)}, s32[]{:S(2)}) async-start(s8[4587520]{0:T(1024)(128)(4,1)} %bitcast.155), calls=%async_computation.4 | async-start | bytes 8388608
  281.6 6.7 %slice-start.5 = ((s8[4587520]{0:T(1024)(128)(4,1)}), s8[393216]{0:T(1024)(128)(4,1)S(1)}, s32[]{:S(2)}) async-start(s8[4587520]{0:T(1024)(128)(4,1)} %bitcast.155), calls=%async_computation.5 | async-start | bytes 786432
  316.6 1.6 copy-start.5
  318.2 112.4 %collective-permute-start.15 = (bf16[640,896]{1,0:T(8,128)(2,1)S(1)}, bf16[640,896]{1,0:T(8,128)(2,1)S(1)}, u32[]{:S(2)}, u32[]{:S(2)}) collective-permute-start(bf16[640,896]{1,0:T(8,128)(2,1)S(1)} %copy-done.5), channel_id=1, source_target_pairs={{0,1},{1,0},{2,3},{3,2},{4,5},{5,4},{6,7},{7,6}} | collective-permute-start | bytes 3440648 | tf_op jit(solution)/shard_map/ppermute | solution.py:408
  321.0 85.3 %collective-permute-start.16 = (bf16[640,896]{1,0:T(8,128)(2,1)S(1)}, bf16[640,896]{1,0:T(8,128)(2,1)S(1)}, u32[]{:S(2)}, u32[]{:S(2)}) collective-permute-start(bf16[640,896]{1,0:T(8,128)(2,1)S(1)} %copy-done.5), channel_id=1, source_target_pairs={{0,2},{1,3},{2,0},{3,1},{4,6},{5,7},{6,4},{7,5}} | collective-permute-start | bytes 3440648 | tf_op jit(solution)/shard_map/ppermute | solution.py:407
  325.0 9.1 %copy-start.6 = (bf16[224,2560]{1,0:T(8,128)(2,1)S(1)}, bf16[224,2560]{1,0:T(8,128)(2,1)}, u32[]{:S(2)}) copy-start(bf16[224,2560]{1,0:T(8,128)(2,1)} %fusion.14) | copy-start | bytes 3440644
  328.3 48.8 %collective-permute-start.1 = (bf16[224,2560]{1,0:T(8,128)(2,1)}, bf16[224,2560]{1,0:T(8,128)(2,1)S(1)}, u32[]{:S(2)}, u32[]{:S(2)}) collective-permute-start(bf16[224,2560]{1,0:T(8,128)(2,1)} %fusion.5), channel_id=1, source_target_pairs={{0,2},{1,3},{2,0},{3,1},{4,6},{5,7},{6,4},{7,5}} | collective-permute-start | bytes 3440648 | tf_op jit(solution)/shard_map/ppermute | solution.py:407
  332.7 47.2 %collective-permute-start.8 = (bf16[224,2560]{1,0:T(8,128)(2,1)}, bf16[224,2560]{1,0:T(8,128)(2,1)S(1)}, u32[]{:S(2)}, u32[]{:S(2)}) collective-permute-start(bf16[224,2560]{1,0:T(8,128)(2,1)} %collective-permute-done.7), channel_id=1, source_target_pairs={{0,1},{1,0},{2,3},{3,2},{4,5},{5,4},{6,7},{7,6}} | collective-permute-start | bytes 3440648 | tf_op jit(solution)/shard_map/ppermute | solution.py:409
  334.1 51.0 %collective-permute-start.9 = (bf16[224,2560]{1,0:T(8,128)(2,1)S(1)}, bf16[224,2560]{1,0:T(8,128)(2,1)S(1)}, u32[]{:S(2)}, u32[]{:S(2)}) collective-permute-start(bf16[224,2560]{1,0:T(8,128)(2,1)S(1)} %copy-done.6), channel_id=1, source_target_pairs={{0,1},{1,0},{2,3},{3,2},{4,5},{5,4},{6,7},{7,6}} | collective-permute-start | bytes 3440648 | tf_op jit(solution)/shard_map/ppermute | solution.py:408
  377.1 28.1 %collective-permute-start.10 = (bf16[224,2560]{1,0:T(8,128)(2,1)S(1)}, bf16[224,2560]{1,0:T(8,128)(2,1)S(1)}, u32[]{:S(2)}, u32[]{:S(2)}) collective-permute-start(bf16[224,2560]{1,0:T(8,128)(2,1)S(1)} %copy-done.6), channel_id=1, source_target_pairs={{0,2},{1,3},{2,0},{3,1},{4,6},{5,7},{6,4},{7,5}} | collective-permute-start | bytes 3440648 | tf_op jit(solution)/shard_map/ppermute | solution.py:407
  379.9 2.8 copy-start.4
  379.9 2.8 collective-permute-start.2
  382.7 45.9 %collective-permute-start.4 = (bf16[224,2560]{1,0:T(8,128)(2,1)S(1)}, bf16[224,2560]{1,0:T(8,128)(2,1)S(1)}, u32[]{:S(2)}, u32[]{:S(2)}) collective-permute-start(bf16[224,2560]{1,0:T(8,128)(2,1)S(1)} %copy-done.4), channel_id=1, source_target_pairs={{0,2},{1,3},{2,0},{3,1},{4,6},{5,7},{6,4},{7,5}} | collective-permute-start | bytes 3440648 | tf_op jit(solution)/shard_map/ppermute | solution.py:407
  385.1 43.5 %collective-permute-start.14 = (bf16[640,896]{1,0:T(8,128)(2,1)}, bf16[640,896]{1,0:T(8,128)(2,1)S(1)}, u32[]{:S(2)}, u32[]{:S(2)}) collective-permute-start(bf16[640,896]{1,0:T(8,128)(2,1)} %collective-permute-done.13), channel_id=1, source_target_pairs={{0,1},{1,0},{2,3},{3,2},{4,5},{5,4},{6,7},{7,6}} | collective-permute-start | bytes 3440648 | tf_op jit(solution)/shard_map/ppermute | solution.py:409
  405.2 24.3 %collective-permute-start.3 = (bf16[224,2560]{1,0:T(8,128)(2,1)S(1)}, bf16[224,2560]{1,0:T(8,128)(2,1)S(1)}, u32[]{:S(2)}, u32[]{:S(2)}) collective-permute-start(bf16[224,2560]{1,0:T(8,128)(2,1)S(1)} %copy-done.4), channel_id=1, source_target_pairs={{0,1},{1,0},{2,3},{3,2},{4,5},{5,4},{6,7},{7,6}} | collective-permute-start | bytes 3440648 | tf_op jit(solution)/shard_map/ppermute | solution.py:408
  406.3 26.0 %collective-permute-start.11 = (bf16[224,2560]{1,0:T(8,128)(2,1)S(1)}, bf16[224,2560]{1,0:T(8,128)(2,1)S(1)}, u32[]{:S(2)}, u32[]{:S(2)}) collective-permute-start(bf16[224,2560]{1,0:T(8,128)(2,1)S(1)} %collective-permute-done.10), channel_id=1, source_target_pairs={{0,1},{1,0},{2,3},{3,2},{4,5},{5,4},{6,7},{7,6}} | collective-permute-start | bytes 3440648 | tf_op jit(solution)/shard_map/ppermute | solution.py:409
  428.6 3.4 collective-permute-start.17
  428.7 4.8 %collective-permute-start.5 = (bf16[224,2560]{1,0:T(8,128)(2,1)S(1)}, bf16[224,2560]{1,0:T(8,128)(2,1)S(1)}, u32[]{:S(2)}, u32[]{:S(2)}) collective-permute-start(bf16[224,2560]{1,0:T(8,128)(2,1)S(1)} %collective-permute-done.4), channel_id=1, source_target_pairs={{0,1},{1,0},{2,3},{3,2},{4,5},{5,4},{6,7},{7,6}} | collective-permute-start | bytes 3440648 | tf_op jit(solution)/shard_map/ppermute | solution.py:409
  432.3 4.3 copy-start.2

commit v2 on v1

--- a/solution.py
+++ b/solution.py
@@ -1,3 +1,5 @@
+import functools
+
 import jax
 import jax.numpy as jnp
 from jax import lax
@@ -43,7 +45,7 @@
 def step_kernel(
     x, dy, wg, wu, wd,
     gg, gu, gd, ss, s0, q0, p0, a0t,
-    a, atr, dh, h, pr, dg, du, da, sq, wgv, wuv, wdv, dwg, dwd, rdg, rdd, isg, isd, irg, ird, owng, ownd, ssg, ssd, nsend, nrecv,
+    a, atr, dh, h, pr, dgu, da, sq, wgu, wdv, dwg, dwd, rdg, rdd, isg, isd, irg, ird, owng, ownd, ssg, ssd, nsend, nrecv,
     isem, wsem, psem, ssem, d2d_send, d2d_recv, ici_send, ici_recv, osem, n_send, n_recv,
 ):
     me = lax.axis_index("dp")
@@ -65,8 +67,8 @@
     def weights(layer, k, slot, all_three):
         if all_three:
             for d in range(GROUP):
-                yield pltpu.make_async_copy(wg.at[layer, :, hidden(d, k)], wgv.at[slot, :, at(d, PIECE)], wsem.at[slot, 4 + d])
-                yield pltpu.make_async_copy(wu.at[layer, :, hidden(d, k)], wuv.at[slot, :, at(d, PIECE)], wsem.at[slot, 8 + d])
+                yield pltpu.make_async_copy(wg.at[layer, :, hidden(d, k)], wgu.at[slot, :, pl.ds(d * PIECE, PIECE)], wsem.at[slot, 4 + d])
+                yield pltpu.make_async_copy(wu.at[layer, :, hidden(d, k)], wgu.at[slot, :, pl.ds(C + d * PIECE, PIECE)], wsem.at[slot, 8 + d])
         for d in range(GROUP):
             yield pltpu.make_async_copy(wd.at[layer, hidden(d, k), :], wdv.at[slot, at(d, PIECE), :], wsem.at[slot, d])
 
@@ -129,8 +131,8 @@
         def _(t):
             r = at(t, TILE)
             step = k * TILES + t
-            gate = dot(a[r, :], wgv[slot])
-            up = dot(a[r, :], wuv[slot])
+            wide = dot(a[r, :], wgu[slot])
+            gate, up = wide[:, :C], wide[:, C:]
             s = logistic(gate)
             silu = gate * s
             prod = (silu * up).astype(BF)
@@ -181,13 +183,11 @@
             dwd[1 - core, half] = out[:PIECE]
             dwd[core, half] = out[PIECE:]
 
-    def gradient(d, i):
-        @pl.loop(0, 2, unroll=True)
-        def _(half):
-            out = dot(atr[at(half, 2 * OWN_D), :], d[...]).astype(BF)
-            rows = slice(i * OWN_D, (i + 1) * OWN_D)
-            dwg[1 - core, half, rows, :] = out[:OWN_D]
-            dwg[core, half, rows, :] = out[OWN_D:]
+    def gradient_wide(half):
+        out = dot(atr[half * 2 * OWN_D : (half + 1) * 2 * OWN_D, :], dgu[...]).astype(BF)
+        for q, where in enumerate((1 - core, core)):
+            for i in range(2):
+                dwg[where, half, i * OWN_D : (i + 1) * OWN_D, :] = out[q * OWN_D : (q + 1) * OWN_D, i * C : (i + 1) * C]
 
     def sum_on_chip(n, part):
         slot, place = n % 2, n % OWNS
@@ -205,9 +205,9 @@
     def gradients(n, slot):
         gradient_down(slot)
         to_near(n, 0).start()
-        gradient(dg, 0)
+        gradient_wide(0)
         sum_on_chip(n, 0)
-        gradient(du, 1)
+        gradient_wide(1)
         to_near(n, 1).start()
 
     def results(n):
@@ -246,15 +246,14 @@
         @pl.loop(0, TILES)
         def _(t):
             r = at(t, TILE)
-            n = a[r, :]
-            gate = dot(n, wgv[slot])
-            up = dot(n, wuv[slot])
+            wide = dot(a[r, :], wgu[slot])
+            gate, up = wide[:, :C], wide[:, C:]
             dp = dot(dh[r, :], wdv[slot], (1, 1)).astype(BF).astype(F32)
             s = logistic(gate)
             silu = gate * s
             pr[0, r, :] = (silu * up).astype(BF)
-            dg[r, :] = (dp * (up * (s * (1.0 + gate * (1.0 - s))))).astype(BF)
-            du[r, :] = (dp * silu).astype(BF)
+            dgu[r, pl.ds(0, C)] = (dp * (up * (s * (1.0 + gate * (1.0 - s))))).astype(BF)
+            dgu[r, pl.ds(C, C)] = (dp * silu).astype(BF)
 
         @pl.when(k >= OWNS)
         def _():
@@ -265,7 +264,7 @@
         @pl.loop(0, TILES)
         def _(t):
             r = at(t, TILE)
-            da[r, :] += dot(dg[r, :], wgv[slot], (1, 1)) + dot(du[r, :], wuv[slot], (1, 1))
+            da[r, :] += dot(dgu[r, :], wgu[slot], (1, 1))
 
         sum_on_chip(k, 1)
 
@@ -304,8 +303,8 @@
             silu_in(k, t).wait()
             factor_in(k, t).wait()
             dp = dot(dh[r, :], wdv[slot], (1, 1)).astype(BF).astype(F32)
-            du[r, :] = (dp * da[r, pl.ds(0, C)]).astype(BF)
-            dg[r, :] = (dp * sq[t // 2, t % 2]).astype(BF)
+            dgu[r, pl.ds(C, C)] = (dp * da[r, pl.ds(0, C)]).astype(BF)
+            dgu[r, pl.ds(0, C)] = (dp * sq[t // 2, t % 2]).astype(BF)
 
         @pl.when(k < CHUNKS - 1)
         def _():
@@ -335,7 +334,10 @@
         wait(results(n))
 
     wait(norms)
-    ss[...] = nsend[...] + nrecv[0] + nrecv[1] + nrecv[2]
+    squares = nsend[...] + nrecv[0] + nrecv[1] + nrecv[2]
+    factor = jnp.minimum(1.0, 0.5 * lax.rsqrt(squares / (6 * D * FF) + 1e-30))
+    for i in range(FF // 128):
+        ss[:, i * 128 : (i + 1) * 128] = factor
 
 
 def gradients_of(*args):
@@ -347,7 +349,7 @@
             jax.ShapeDtypeStruct((2, OWN_D, FF), BF),
             jax.ShapeDtypeStruct((2, OWN_D, FF), BF),
             jax.ShapeDtypeStruct((2, OWN_F, D), BF),
-            jax.ShapeDtypeStruct((8, 128), F32),
+            jax.ShapeDtypeStruct((8, FF), F32),
             jax.ShapeDtypeStruct((CHUNKS, T, C), F32),
             jax.ShapeDtypeStruct((CHUNKS, T, C), F32),
             jax.ShapeDtypeStruct((CHUNKS, T, C), BF),
@@ -357,8 +359,8 @@
         out_specs=[ANY] * 3 + [pl.BlockSpec(memory_space=pltpu.VMEM)] + [ANY] * 4,
         scratch_shapes=[
             vmem((T, D), BF), vmem((D, T), BF), vmem((T, D), BF), vmem((T, D), BF),
-            vmem((2, T, C), BF), vmem((T, C), BF), vmem((T, C), BF), vmem((T, D), F32), vmem((2, 2, TILE, C), F32),
-            vmem((2, D, C), BF), vmem((2, D, C), BF), vmem((2, C, D), BF),
+            vmem((2, T, C), BF), vmem((T, 2 * C), BF), vmem((T, D), F32), vmem((2, 2, TILE, C), F32),
+            vmem((2, D, 2 * C), BF), vmem((2, C, D), BF),
             vmem((2, 2, g_rows, C), BF), vmem((2, 2, PIECE, D), BF),
             vmem((2, 2, g_rows, C), BF), vmem((2, 2, PIECE, D), BF),
             vmem((SENDS, g_rows, C), BF), vmem((SENDS, PIECE, D), BF),
@@ -375,6 +377,40 @@
     )(*args)[:4]
 
 
+def places(shapes):
+    space = pl.BlockSpec(memory_space=pltpu.HBM)
+    return list(pl.pallas_call(lambda *_: None, out_shape=[jax.ShapeDtypeStruct(s, BF) for s in shapes], out_specs=[space] * len(shapes), name="places")())
+
+
+def place_kernel(layer, which, part, _, out, tile, sem):
+    me = lax.axis_index("dp")
+    block = (me, me + 1 - 2 * (me % 2), (me + 2) % 4, 3 - me)[which]
+    rows = part.shape[0] // 4
+    ins = [pltpu.make_async_copy(part.at[pl.ds(i * rows, rows)], tile.at[pl.ds(i * rows, rows)], sem.at[0, i]) for i in range(4)]
+    outs = [pltpu.make_async_copy(tile.at[pl.ds(i * rows, rows)], out.at[layer, block, pl.ds(i * rows, rows)], sem.at[1, i]) for i in range(4)]
+    for c in ins:
+        c.start()
+    for i, o in zip(ins, outs, strict=True):
+        i.wait()
+        o.start()
+    for c in outs:
+        c.wait()
+
+
+def place(out, part, layer, which):
+    space = pl.BlockSpec(memory_space=pltpu.HBM)
+    return pl.pallas_call(
+        functools.partial(place_kernel, layer, which),
+        out_shape=jax.ShapeDtypeStruct(out.shape, out.dtype),
+        in_specs=[ANY, space],
+        out_specs=space,
+        scratch_shapes=[pltpu.VMEM(part.shape, part.dtype), pltpu.SemaphoreType.DMA((2, 4))],
+        input_output_aliases={1: 0},
+        cost_estimate=pl.CostEstimate(flops=part.size, bytes_accessed=4 * part.size, transcendentals=0),
+        name="place",
+    )(part, out)
+
+
 def solution(mesh):
     far = [(d, d ^ 2) for d in range(GROUP)]
     near = [(d, d ^ 1) for d in range(GROUP)]
@@ -382,37 +418,38 @@
     def step(x, dy, *arrays):
         weights, ms, vs = (arrays[i : i + 3] for i in (0, 3, 6))
         me = lax.axis_index("dp")
-        *gradients, squares = gradients_of(x, dy, *weights)
-        count = sum(w.size for w in weights)
-        factor = jnp.minimum(1.0, 0.5 * lax.rsqrt(squares[0, 0] / count + 1e-30))
+        *gradients, factors = gradients_of(x, dy, *weights)
 
         def adamw(w, m, v, g, factor):
-            g = g.astype(F32) * factor
+            g = g.astype(F32) * factor[:1, : g.shape[-1]]
             m = 0.9 * m + 0.1 * g
             v = 0.95 * v + 0.05 * g * g
             return (w.astype(F32) - 0.02 * (m * lax.rsqrt(v + 1e-8) + 0.1 * w.astype(F32))).astype(BF), m, v
 
-        mine = []
-        for w, g in zip(weights, gradients, strict=True):
-            mine.append(lax.dynamic_index_in_dim(w.reshape(g.shape[0], GROUP, *g.shape[1:]), me, 1, keepdims=False))
-        units = [(i, layer) for i in range(3) for layer in range(2)]
+        units = [(0, 0, 0, 112), (0, 0, 112, 112)] + [(i, layer, 0, gradients[i].shape[1]) for i in range(3) for layer in range(2)][1:]
         blocks = {}
-        for i, layer in units:
-            block = adamw(mine[i][layer], ms[i][layer], vs[i][layer], gradients[i][layer], factor)[0]
-            block, factor = lax.optimization_barrier((block, factor))
-            blocks[i, layer] = block
-        out = [jnp.zeros((g.shape[0], GROUP, *g.shape[1:]), BF) for g in gradients]
-        for i, layer in units:
-            block = blocks[i, layer]
+        for u, (i, layer, first, rows) in enumerate(units):
+            g = gradients[i]
+            whole = weights[i].reshape(g.shape[0], GROUP, *g.shape[1:])
+            w = lax.dynamic_slice(whole, (layer, me, first, 0), (1, 1, rows, g.shape[2]))[0, 0]
+            block = adamw(w, *(t[i][layer, first : first + rows] for t in (ms, vs, gradients)), factors)[0]
+            block, factors = lax.optimization_barrier((block, factors))
+            blocks[u] = block
+        out = places([(g.shape[0], GROUP, *g.shape[1:]) for g in gradients])
+        for u, (i, layer, first, rows) in enumerate(units):
+            block = blocks[u]
             of_far = lax.ppermute(block, "dp", far)
             of_near = lax.ppermute(block, "dp", near)
             of_across = lax.ppermute(of_far, "dp", near)
-            for which, part in ((me, block), (me ^ 1, of_near), (me ^ 2, of_far), (me ^ 3, of_across)):
-                out[i] = lax.dynamic_update_slice(out[i], part[None, None], (layer, which, 0, 0))
+            for which, part in enumerate((block, of_near, of_far, of_across)):
+                if i == 2:
+                    out[i] = place(out[i], part, layer, which)
+                else:
+                    out[i] = lax.dynamic_update_slice(out[i], part[None, None], (layer, me ^ which, first, 0))
         new_w = [o.reshape(w.shape) for o, w in zip(out, weights, strict=True)]
         new_m, new_v = [], []
-        for own, m, v, g in zip(mine, ms, vs, gradients, strict=True):
-            _, m, v = adamw(own, m, v, g, factor)
+        for m, v, g in zip(ms, vs, gradients, strict=True):
+            _, m, v = adamw(jnp.zeros((), BF), m, v, g, factors)
             new_m.append(m)
             new_v.append(v)
         return (*new_w, *new_m, *new_v)

time: 437 us -> 445 us (1.018)
  Pallas kernels: 249 us -> 266 us
  local copies, waits for them, and re-layouts: 42.3 us -> 35.2 us
  waiting for transfers between devices: 85.7 us -> 80.8 us
    pallas_call x0 -> x9, Pallas kernels: none -> 16.3 us  [the longest x8 16.3 us: place(): pl.pallas_call(functools.partial(place_kernel, layer, which), out_shape=j...]
    another operation x2 -> x0, local copies, waits for them, and re-layouts: 8.87 us -> none
    ppermute x6 -> x7, waiting for transfers between devices: 85.1 us -> 80.7 us  [step(): of_far = lax.ppermute(block, 'dp', far)]
    dynamic_update_slice x24 -> x20, local copies, waits for them, and re-layouts: 29.4 us -> 32.8 us  [step(): lax.dynamic_update_slice(out[i], part[None, None], (layer, me ^ which, fi...]
    ppermute x6 -> x7, starting transfers between devices: 8.43 us -> 10.5 us  [step(): of_far = lax.ppermute(block, 'dp', far)]
    convert_element_type x6 -> x7, other arithmetic: 26.7 us -> 25.5 us  [adamw(): (w.astype(F32) - 0.02 * (m * lax.rsqrt(v + 1e-08) + 0.1 * w.astype(F32)))...]
  transfers between devices with their start and end apart: 18 -> 21, of which waited for: 5 -> 5; matrix products, arithmetic and copies ran while one was open for 14% -> 13% of each run, Pallas kernels for 0% -> 4%
where the time goes in v2:
time: 445 us; the launch traced here: 444 us
  Pallas kernels  266 us (60%)
  waiting for transfers between devices  80.8 us (18%)
  other arithmetic  48.8 us (11%)
  local copies, waits for them, and re-layouts  35.2 us (8%)
  starting transfers between devices  12.9 us (3%)
    pallas_call x1, Pallas kernels, gradients_of(): pl.pallas_call(step_kernel, out_shape=[jax.ShapeDtypeStruct((2, OWN_D, FF...  249 us
    ppermute x7, waiting for transfers between devices, step(): of_far = lax.ppermute(block, 'dp', far)  80.7 us
    dynamic_update_slice x20, local copies, waits for them, and re-layouts, step(): lax.dynamic_update_slice(out[i], part[None, None], (layer, me ^ which, fi...  32.8 us
    convert_element_type x7, other arithmetic, adamw(): (w.astype(F32) - 0.02 * (m * lax.rsqrt(v + 1e-08) + 0.1 * w.astype(F32)))...  25.5 us
    add x2, other arithmetic, adamw(): v = 0.95 * v + 0.05 * g * g  23.3 us
    pallas_call x8, Pallas kernels, place(): pl.pallas_call(functools.partial(place_kernel, layer, which), out_shape=j...  16.3 us
    ppermute x7, starting transfers between devices, step(): of_far = lax.ppermute(block, 'dp', far)  10.5 us
  transfers between devices with their start and end apart: 21, of which 5 were waited for; matrix products, arithmetic and copies ran while one was open for 13% of the time, Pallas kernels for 4%

profile of v2, /device:TPU:0, one launch (start us, length us, event | category | flops | bytes accessed | tf_op | source)
XLA Modules:
  0.0 444.3 jit_solution(9002851371778351800)
XLA Ops:
  0.6 249.3 %gradients.1 = (bf16[2,224,2560]{2,1,0:T(8,128)(2,1)}, bf16[2,224,2560]{2,1,0:T(8,128)(2,1)}, bf16[2,640,896]{2,1,0:T(8,128)(2,1)}, f32[8,2560]{1,0:T(8,128)}, f...) custom-call(bf16[1,2048,896]{2,1,0:T(8,128)(2,1)} %x.1, ...), custom_call_target="tpu_custom_call" | custom-call | flops 140928614400 | bytes 200000000 | tf_op jit(solution)/shard_map/gradients/pallas_call | solution.py:346
  250.0 1.1 slice_reduce_fusion.5
  251.1 3.5 fusion.50
  254.7 0.0 slice-start
  254.7 3.4 fusion.53
  258.1 0.0 slice-start.1
  258.1 4.4 fusion.5
  262.6 0.0 slice-start.2
  262.6 0.0 slice-start.4
  262.6 4.1 fusion.8
  266.8 3.8 fusion.11
  270.6 3.7 fusion.14.part
  274.3 2.4 collective-permute-start.18
  276.7 0.1 collective-permute-start
  276.8 0.3 collective-permute-start.1
  277.1 2.6 fusion.17.part
  279.7 0.1 collective-permute-start.17
  279.9 14.6 %fusion.1 = (f32[2,224,2560]{2,1,0:T(8,128)}, f32[2,224,2560]{2,1,0:T(8,128)}, f32[2,224,2560]{2,1,0:T(8,128)}, f32[2,224,2560]{2,1,0:T(8,128)}) fusion(f32[2,224,2560]{2,1,0:T(8,128)} %param.20, bf16[2,224,2560]{2,1,0:T(8,128)(2,1)} %get-tuple-element.39, f32[2560]{0:T(1024)S(1)} %slice_reduce_fusion, f32[2,224,2560]{2,1,0:T(8,128)} %param.17, ...), kind=kLoop, calls=%fused_computation.4 | loop fusion | flops 20643840 | bytes 41297920 | tf_op jit(solution)/shard_map/add | solution.py:426
  294.5 2.2 place.8._
  296.7 8.7 %fusion.2 = (f32[2,640,896]{2,1,0:T(8,128)}, f32[2,640,896]{2,1,0:T(8,128)}) fusion(f32[2,640,896]{2,1,0:T(8,128)} %param.21, bf16[2,640,896]{2,1,0:T(8,128)(2,1)S(1)} %copy-done.4, f32[896]{0:T(1024)S(1)} %slice_reduce_fusion.6, f32[2,640,896]{2,1,0:T(8,128)} %param.18), kind=kLoop, calls=%fused_computation.5 | loop fusion | flops 10321920 | bytes 20647424 | tf_op jit(solution)/shard_map/add | solution.py:426
  305.4 2.3 bitcast_dynamic-update-slice_fusion.7
  307.7 1.9 bitcast_dynamic-update-slice_fusion.19
  309.7 1.7 collective-permute-start.15
  311.4 4.0 collective-permute-done.1
  315.4 1.9 bitcast_dynamic-update-slice_fusion.18
  317.3 1.9 bitcast_dynamic-update-slice_fusion.17
  319.2 0.5 collective-permute-start.9
  319.7 2.0 place.9._
  321.8 0.1 collective-permute-start.3
  321.8 2.0 place.10._
  323.9 2.0 collective-permute-start.4
  325.9 0.8 bitcast_dynamic-update-slice_fusion.16
  326.8 0.8 bitcast_dynamic-update-slice_fusion.15
  327.6 0.0 collective-permute-start.10
  327.7 24.5 %collective-permute-done.4 = bf16[112,2560]{1,0:T(8,128)(2,1)S(1)} collective-permute-done((bf16[112,2560]{1,0:T(8,128)(2,1)S(1)}, bf16[112,2560]{1,0:T(8,128)(2,1)S(1)}, u32[]{:S(2)}, u32[]{:S(2)}) %collective-permute-start.4) | collective-permute-done | bytes 573472 | tf_op jit(solution)/shard_map/ppermute | solution.py:441
  352.1 1.9 bitcast_dynamic-update-slice_fusion.14
  354.0 0.8 bitcast_dynamic-update-slice_fusion.13
  354.9 0.5 collective-permute-start.6
  355.4 0.8 bitcast_dynamic-update-slice_fusion.12
  356.3 1.1 bitcast_dynamic-update-slice_fusion.11
  357.3 2.0 collective-permute-start.7
  359.4 2.3 bitcast_dynamic-update-slice_fusion.6
  361.7 15.1 %collective-permute-done.10 = bf16[224,2560]{1,0:T(8,128)(2,1)} collective-permute-done((bf16[224,2560]{1,0:T(8,128)(2,1)}, bf16[224,2560]{1,0:T(8,128)(2,1)}, u32[]{:S(2)}, u32[]{:S(2)}) %collective-permute-start.10) | collective-permute-done | bytes 1146912 | tf_op jit(solution)/shard_map/ppermute | solution.py:441
  376.8 2.0 collective-permute-start.13
  378.8 2.3 bitcast_dynamic-update-slice_fusion.5
  381.2 0.5 collective-permute-start.11
  381.7 19.6 %collective-permute-done.7 = bf16[224,2560]{1,0:T(8,128)(2,1)S(1)} collective-permute-done((bf16[224,2560]{1,0:T(8,128)(2,1)S(1)}, bf16[224,2560]{1,0:T(8,128)(2,1)S(1)}, u32[]{:S(2)}, u32[]{:S(2)}) %collective-permute-start.7) | collective-permute-done | bytes 1146912 | tf_op jit(solution)/shard_map/ppermute | solution.py:441
  401.3 1.1 bitcast_dynamic-update-slice_fusion.10
  402.4 1.1 bitcast_dynamic-update-slice_fusion.9
  403.5 0.4 collective-permute-start.12
  404.0 2.0 place.11._
  406.0 2.0 place.12._
  408.0 0.1 collective-permute-start.8
  408.1 17.6 %collective-permute-done.13 = bf16[224,2560]{1,0:T(8,128)(2,1)} collective-permute-done((bf16[224,2560]{1,0:T(8,128)(2,1)S(1)}, bf16[224,2560]{1,0:T(8,128)(2,1)}, u32[]{:S(2)}, u32[]{:S(2)}) %collective-permute-start.13) | collective-permute-done | bytes 1146912 | tf_op jit(solution)/shard_map/ppermute | solution.py:441
  425.7 2.0 place.13._
  427.7 2.0 place.14._
  429.8 1.0 copy-done.10
  430.8 2.0 place.15
  432.8 2.3 bitcast_dynamic-update-slice_fusion.4
  435.2 1.1 bitcast_dynamic-update-slice_fusion.3
  436.3 2.3 bitcast_dynamic-update-slice_fusion.2
  438.6 2.3 bitcast_dynamic-update-slice_fusion.1
  440.9 2.3 bitcast_dynamic-update-slice_fusion
  443.3 1.1 bitcast_dynamic-update-slice_fusion.8
  (67 shorter events, 0.3 us)
Async XLA Ops:
  250.0 4.7 %copy-start.12 = (f32[8,2560]{1,0:T(8,128)S(1)}, f32[8,2560]{1,0:T(8,128)}, u32[]{:S(2)}) copy-start(f32[8,2560]{1,0:T(8,128)} %get-tuple-element.50) | copy-start | bytes 245764
  250.0 4.7 %copy-start.2 = (bf16[2,224,2560]{2,1,0:T(8,128)(2,1)S(1)}, bf16[2,224,2560]{2,1,0:T(8,128)(2,1)}, u32[]{:S(2)}) copy-start(bf16[2,224,2560]{2,1,0:T(8,128)(2,1)} %get-tuple-element.31) | copy-start | bytes 6881284
  251.1 7.0 %copy-start = (f32[2,224,2560]{2,1,0:T(8,128)S(1)}, f32[2,224,2560]{2,1,0:T(8,128)}, u32[]{:S(2)}) copy-start(f32[2,224,2560]{2,1,0:T(8,128)} %param.19) | copy-start | bytes 13762564
  254.7 7.9 %slice-start = ((s8[4587520]{0:T(1024)(128)(4,1)}), s8[4194304]{0:T(1024)(128)(4,1)S(1)}, s32[]{:S(2)}) async-start(s8[4587520]{0:T(1024)(128)(4,1)} %bitcast.117), calls=%async_computation | async-start | bytes 8388608
  258.1 4.5 %slice-start.1 = ((s8[4587520]{0:T(1024)(128)(4,1)}), s8[393216]{0:T(1024)(128)(4,1)S(1)}, s32[]{:S(2)}) async-start(s8[4587520]{0:T(1024)(128)(4,1)} %bitcast.117), calls=%async_computation.1 | async-start | bytes 786432
  258.1 4.5 %copy-start.1 = (f32[2,224,2560]{2,1,0:T(8,128)S(1)}, f32[2,224,2560]{2,1,0:T(8,128)}, u32[]{:S(2)}) copy-start(f32[2,224,2560]{2,1,0:T(8,128)} %param.17) | copy-start | bytes 13762564
  258.1 8.7 %copy-start.5 = (bf16[2,224,2560]{2,1,0:T(8,128)(2,1)S(1)}, bf16[2,224,2560]{2,1,0:T(8,128)(2,1)}, u32[]{:S(2)}) copy-start(bf16[2,224,2560]{2,1,0:T(8,128)(2,1)} %get-tuple-element.39) | copy-start | bytes 6881284
  262.6 8.0 %slice-start.2 = ((s8[4587520]{0:T(1024)(128)(4,1)}), s8[4194304]{0:T(1024)(128)(4,1)S(1)}, s32[]{:S(2)}) async-start(s8[4587520]{0:T(1024)(128)(4,1)} %bitcast.119), calls=%async_computation.2 | async-start | bytes 8388608
  262.6 7.9 %slice-start.4 = ((s8[4587520]{0:T(1024)(128)(4,1)}), s8[4194304]{0:T(1024)(128)(4,1)S(1)}, s32[]{:S(2)}) async-start(s8[4587520]{0:T(1024)(128)(4,1)} %bitcast.121), calls=%async_computation.4 | async-start | bytes 8388608
  266.7 3.9 slice-start.3
  266.7 3.9 slice-start.5
  266.8 3.8 copy-start.3
  274.3 44.9 %collective-permute-start.20 = (bf16[640,896]{1,0:T(8,128)(2,1)}, bf16[640,896]{1,0:T(8,128)(2,1)}, u32[]{:S(2)}, u32[]{:S(2)}) collective-permute-start(bf16[640,896]{1,0:T(8,128)(2,1)} %fusion.14.part), channel_id=1, source_target_pairs={{0,1},{1,0},{2,3},{3,2},{4,5},{5,4},{6,7},{7,6}} | collective-permute-start | bytes 3440648 | tf_op jit(solution)/shard_map/ppermute | solution.py:442
  274.3 47.4 %collective-permute-start.18 = (bf16[640,896]{1,0:T(8,128)(2,1)}, bf16[640,896]{1,0:T(8,128)(2,1)}, u32[]{:S(2)}, u32[]{:S(2)}) collective-permute-start(bf16[640,896]{1,0:T(8,128)(2,1)} %fusion.14.part), channel_id=1, source_target_pairs={{0,2},{1,3},{2,0},{3,1},{4,6},{5,7},{6,4},{7,5}} | collective-permute-start | bytes 3440648 | tf_op jit(solution)/shard_map/ppermute | solution.py:441
  276.7 33.0 %collective-permute-start = (bf16[112,2560]{1,0:T(8,128)(2,1)}, bf16[112,2560]{1,0:T(8,128)(2,1)}, u32[]{:S(2)}, u32[]{:S(2)}) collective-permute-start(bf16[112,2560]{1,0:T(8,128)(2,1)} %fusion.50), channel_id=1, source_target_pairs={{0,1},{1,0},{2,3},{3,2},{4,5},{5,4},{6,7},{7,6}} | collective-permute-start | bytes 1720328 | tf_op jit(solution)/shard_map/ppermute | solution.py:442
  276.8 38.6 %collective-permute-start.1 = (bf16[112,2560]{1,0:T(8,128)(2,1)}, bf16[112,2560]{1,0:T(8,128)(2,1)}, u32[]{:S(2)}, u32[]{:S(2)}) collective-permute-start(bf16[112,2560]{1,0:T(8,128)(2,1)} %fusion.50), channel_id=1, source_target_pairs={{0,2},{1,3},{2,0},{3,1},{4,6},{5,7},{6,4},{7,5}} | collective-permute-start | bytes 1720328 | tf_op jit(solution)/shard_map/ppermute | solution.py:441
  279.7 30.0 %copy-start.6 = (bf16[640,896]{1,0:T(8,128)(2,1)}, bf16[640,896]{1,0:T(8,128)(2,1)S(1)}, u32[]{:S(2)}) copy-start(bf16[640,896]{1,0:T(8,128)(2,1)S(1)} %fusion.17.part) | copy-start | bytes 3440644
  279.7 128.4 %collective-permute-start.17 = (bf16[640,896]{1,0:T(8,128)(2,1)S(1)}, bf16[640,896]{1,0:T(8,128)(2,1)}, u32[]{:S(2)}, u32[]{:S(2)}) collective-permute-start(bf16[640,896]{1,0:T(8,128)(2,1)S(1)} %fusion.17.part), channel_id=1, source_target_pairs={{0,1},{1,0},{2,3},{3,2},{4,5},{5,4},{6,7},{7,6}} | collective-permute-start | bytes 3440648 | tf_op jit(solution)/shard_map/ppermute | solution.py:442
  294.5 2.2 copy-start.4
  309.7 71.5 %collective-permute-start.15 = (bf16[640,896]{1,0:T(8,128)(2,1)S(1)}, bf16[640,896]{1,0:T(8,128)(2,1)}, u32[]{:S(2)}, u32[]{:S(2)}) collective-permute-start(bf16[640,896]{1,0:T(8,128)(2,1)S(1)} %fusion.17.part), channel_id=1, source_target_pairs={{0,2},{1,3},{2,0},{3,1},{4,6},{5,7},{6,4},{7,5}} | collective-permute-start | bytes 3440648 | tf_op jit(solution)/shard_map/ppermute | solution.py:441
  315.4 8.5 %collective-permute-start.2 = (bf16[112,2560]{1,0:T(8,128)(2,1)}, bf16[112,2560]{1,0:T(8,128)(2,1)S(1)}, u32[]{:S(2)}, u32[]{:S(2)}) collective-permute-start(bf16[112,2560]{1,0:T(8,128)(2,1)} %collective-permute-done.1), channel_id=1, source_target_pairs={{0,1},{1,0},{2,3},{3,2},{4,5},{5,4},{6,7},{7,6}} | collective-permute-start | bytes 1720328 | tf_op jit(solution)/shard_map/ppermute | solution.py:443
  319.2 2.6 copy-start.9
  319.2 38.1 %collective-permute-start.9 = (bf16[224,2560]{1,0:T(8,128)(2,1)}, bf16[224,2560]{1,0:T(8,128)(2,1)}, u32[]{:S(2)}, u32[]{:S(2)}) collective-permute-start(bf16[224,2560]{1,0:T(8,128)(2,1)} %fusion.8), channel_id=1, source_target_pairs={{0,1},{1,0},{2,3},{3,2},{4,5},{5,4},{6,7},{7,6}} | collective-permute-start | bytes 3440648 | tf_op jit(solution)/shard_map/ppermute | solution.py:442
  321.8 5.9 %collective-permute-start.3 = (bf16[112,2560]{1,0:T(8,128)(2,1)S(1)}, bf16[112,2560]{1,0:T(8,128)(2,1)}, u32[]{:S(2)}, u32[]{:S(2)}) collective-permute-start(bf16[112,2560]{1,0:T(8,128)(2,1)S(1)} %copy-done.9), channel_id=1, source_target_pairs={{0,1},{1,0},{2,3},{3,2},{4,5},{5,4},{6,7},{7,6}} | collective-permute-start | bytes 1720328 | tf_op jit(solution)/shard_map/ppermute | solution.py:442
  323.9 31.0 %copy-start.8 = (bf16[224,2560]{1,0:T(8,128)(2,1)S(1)}, bf16[224,2560]{1,0:T(8,128)(2,1)}, u32[]{:S(2)}) copy-start(bf16[224,2560]{1,0:T(8,128)(2,1)} %fusion.5) | copy-start | bytes 3440644
  323.9 28.2 %collective-permute-start.4 = (bf16[112,2560]{1,0:T(8,128)(2,1)S(1)}, bf16[112,2560]{1,0:T(8,128)(2,1)S(1)}, u32[]{:S(2)}, u32[]{:S(2)}) collective-permute-start(bf16[112,2560]{1,0:T(8,128)(2,1)S(1)} %copy-done.9), channel_id=1, source_target_pairs={{0,2},{1,3},{2,0},{3,1},{4,6},{5,7},{6,4},{7,5}} | collective-permute-start | bytes 1720328 | tf_op jit(solution)/shard_map/ppermute | solution.py:441
  327.6 49.2 %collective-permute-start.10 = (bf16[224,2560]{1,0:T(8,128)(2,1)}, bf16[224,2560]{1,0:T(8,128)(2,1)}, u32[]{:S(2)}, u32[]{:S(2)}) collective-permute-start(bf16[224,2560]{1,0:T(8,128)(2,1)} %fusion.8), channel_id=1, source_target_pairs={{0,2},{1,3},{2,0},{3,1},{4,6},{5,7},{6,4},{7,5}} | collective-permute-start | bytes 3440648 | tf_op jit(solution)/shard_map/ppermute | solution.py:441
  352.1 2.8 collective-permute-start.5
  354.9 26.3 %collective-permute-start.6 = (bf16[224,2560]{1,0:T(8,128)(2,1)S(1)}, bf16[224,2560]{1,0:T(8,128)(2,1)S(1)}, u32[]{:S(2)}, u32[]{:S(2)}) collective-permute-start(bf16[224,2560]{1,0:T(8,128)(2,1)S(1)} %copy-done.8), channel_id=1, source_target_pairs={{0,1},{1,0},{2,3},{3,2},{4,5},{5,4},{6,7},{7,6}} | collective-permute-start | bytes 3440648 | tf_op jit(solution)/shard_map/ppermute | solution.py:442
  356.3 20.6 %copy-start.7 = (bf16[224,2560]{1,0:T(8,128)(2,1)S(1)}, bf16[224,2560]{1,0:T(8,128)(2,1)}, u32[]{:S(2)}) copy-start(bf16[224,2560]{1,0:T(8,128)(2,1)} %fusion.11) | copy-start | bytes 3440644
  357.3 44.0 %collective-permute-start.7 = (bf16[224,2560]{1,0:T(8,128)(2,1)S(1)}, bf16[224,2560]{1,0:T(8,128)(2,1)S(1)}, u32[]{:S(2)}, u32[]{:S(2)}) collective-permute-start(bf16[224,2560]{1,0:T(8,128)(2,1)S(1)} %copy-done.8), channel_id=1, source_target_pairs={{0,2},{1,3},{2,0},{3,1},{4,6},{5,7},{6,4},{7,5}} | collective-permute-start | bytes 3440648 | tf_op jit(solution)/shard_map/ppermute | solution.py:441
  376.8 48.9 %collective-permute-start.13 = (bf16[224,2560]{1,0:T(8,128)(2,1)S(1)}, bf16[224,2560]{1,0:T(8,128)(2,1)}, u32[]{:S(2)}, u32[]{:S(2)}) collective-permute-start(bf16[224,2560]{1,0:T(8,128)(2,1)S(1)} %copy-done.7), channel_id=1, source_target_pairs={{0,2},{1,3},{2,0},{3,1},{4,6},{5,7},{6,4},{7,5}} | collective-permute-start | bytes 3440648 | tf_op jit(solution)/shard_map/ppermute | solution.py:441
  381.2 22.3 %collective-permute-start.19 = (bf16[640,896]{1,0:T(8,128)(2,1)}, bf16[640,896]{1,0:T(8,128)(2,1)}, u32[]{:S(2)}, u32[]{:S(2)}) collective-permute-start(bf16[640,896]{1,0:T(8,128)(2,1)} %collective-permute-done.18.part), channel_id=1, source_target_pairs={{0,1},{1,0},{2,3},{3,2},{4,5},{5,4},{6,7},{7,6}} | collective-permute-start | bytes 3440648 | tf_op jit(solution)/shard_map/ppermute | solution.py:443
  381.2 51.6 %collective-permute-start.11 = (bf16[224,2560]{1,0:T(8,128)(2,1)}, bf16[224,2560]{1,0:T(8,128)(2,1)}, u32[]{:S(2)}, u32[]{:S(2)}) collective-permute-start(bf16[224,2560]{1,0:T(8,128)(2,1)} %collective-permute-done.10), channel_id=1, source_target_pairs={{0,1},{1,0},{2,3},{3,2},{4,5},{5,4},{6,7},{7,6}} | collective-permute-start | bytes 3440648 | tf_op jit(solution)/shard_map/ppermute | solution.py:443
  401.3 2.2 copy-start.11
  401.3 28.5 %collective-permute-start.16 = (bf16[640,896]{1,0:T(8,128)(2,1)}, bf16[640,896]{1,0:T(8,128)(2,1)S(1)}, u32[]{:S(2)}, u32[]{:S(2)}) collective-permute-start(bf16[640,896]{1,0:T(8,128)(2,1)} %collective-permute-done.15.part), channel_id=1, source_target_pairs={{0,1},{1,0},{2,3},{3,2},{4,5},{5,4},{6,7},{7,6}} | collective-permute-start | bytes 3440648 | tf_op jit(solution)/shard_map/ppermute | solution.py:443
  403.5 32.7 %collective-permute-start.12 = (bf16[224,2560]{1,0:T(8,128)(2,1)S(1)}, bf16[224,2560]{1,0:T(8,128)(2,1)}, u32[]{:S(2)}, u32[]{:S(2)}) collective-permute-start(bf16[224,2560]{1,0:T(8,128)(2,1)S(1)} %copy-done.7), channel_id=1, source_target_pairs={{0,1},{1,0},{2,3},{3,2},{4,5},{5,4},{6,7},{7,6}} | collective-permute-start | bytes 3440648 | tf_op jit(solution)/shard_map/ppermute | solution.py:442
  408.0 35.2 %collective-permute-start.8 = (bf16[224,2560]{1,0:T(8,128)(2,1)}, bf16[224,2560]{1,0:T(8,128)(2,1)S(1)}, u32[]{:S(2)}, u32[]{:S(2)}) collective-permute-start(bf16[224,2560]{1,0:T(8,128)(2,1)} %copy-done.11), channel_id=1, source_target_pairs={{0,1},{1,0},{2,3},{3,2},{4,5},{5,4},{6,7},{7,6}} | collective-permute-start | bytes 3440648 | tf_op jit(solution)/shard_map/ppermute | solution.py:443
  425.7 15.2 %collective-permute-start.14 = (bf16[224,2560]{1,0:T(8,128)(2,1)}, bf16[224,2560]{1,0:T(8,128)(2,1)}, u32[]{:S(2)}, u32[]{:S(2)}) collective-permute-start(bf16[224,2560]{1,0:T(8,128)(2,1)} %collective-permute-done.13), channel_id=1, source_target_pairs={{0,1},{1,0},{2,3},{3,2},{4,5},{5,4},{6,7},{7,6}} | collective-permute-start | bytes 3440648 | tf_op jit(solution)/shard_map/ppermute | solution.py:443
  429.8 1.0 copy-start.10

commit v3 on v2

--- a/solution.py
+++ b/solution.py
@@ -46,7 +46,7 @@
     x, dy, wg, wu, wd,
     gg, gu, gd, ss, s0, q0, p0, a0t,
     a, atr, dh, h, pr, dgu, da, sq, wgu, wdv, dwg, dwd, rdg, rdd, isg, isd, irg, ird, owng, ownd, ssg, ssd, nsend, nrecv,
-    isem, wsem, psem, ssem, d2d_send, d2d_recv, ici_send, ici_recv, osem, n_send, n_recv,
+    isem, xsem, wsem, psem, ssem, d2d_send, d2d_recv, ici_send, ici_recv, osem, n_send, n_recv,
 ):
     me = lax.axis_index("dp")
     core, chip = me % 2, me // 2
@@ -88,19 +88,23 @@
     def factor_in(k, t):
         return pltpu.make_async_copy(q0.at[k, at(t, TILE), :], sq.at[t // 2, t % 2], ssem.at[1, t])
 
-    first = [pltpu.make_async_copy(src.at[0], dst, isem.at[i]) for i, (src, dst) in enumerate(((x, h), (dy, dh)))]
-    start(first)
+    def x_in(t):
+        return pltpu.make_async_copy(x.at[0, at(t, 256), :], h.at[at(t, 256), :], xsem.at[t])
+
+    start(x_in(t) for t in range(T // 256))
     start(weights(0, 0, 0, True))
+    dy_in = pltpu.make_async_copy(dy.at[0], dh, isem.at[1])
+    dy_in.start()
     barrier = pltpu.get_barrier_semaphore()
     for to in (near, far, across):
         pl.semaphore_signal(barrier, inc=1, device_id={"dp": to}, device_id_type=pl.DeviceIdType.MESH)
     ssg[...] = jnp.zeros_like(ssg)
     ssd[...] = jnp.zeros_like(ssd)
-    first[0].wait()
 
     @pl.loop(0, T // 256)
     def _(t):
         r = at(t, 256)
+        x_in(t).wait()
         n = normed(h[r, :])
         a[r, :] = n
         atr[:, r] = n.T
@@ -149,7 +153,7 @@
 
         product_out(k).start()
 
-    first[1].wait()
+    dy_in.wait()
     turned.wait()
 
     @pl.loop(0, T // 256)
@@ -205,6 +209,11 @@
     def gradients(n, slot):
         gradient_down(slot)
         to_near(n, 0).start()
+
+        @pl.when(n >= OWNS)
+        def _():
+            finish(n - OWNS)
+
         gradient_wide(0)
         sum_on_chip(n, 0)
         gradient_wide(1)
@@ -255,10 +264,6 @@
             dgu[r, pl.ds(0, C)] = (dp * (up * (s * (1.0 + gate * (1.0 - s))))).astype(BF)
             dgu[r, pl.ds(C, C)] = (dp * silu).astype(BF)
 
-        @pl.when(k >= OWNS)
-        def _():
-            finish(k - OWNS)
-
         gradients(k, 0)
 
         @pl.loop(0, TILES)
@@ -272,16 +277,17 @@
     turned = pltpu.make_async_copy(a0t, atr, isem.at[2])
     turned.start()
 
-    @pl.loop(0, T // 256)
+    @pl.loop(0, TILES)
     def _(t):
-        r = at(t, 256)
-        wide = h[r, :].astype(F32)
-        scale = lax.rsqrt(jnp.mean(wide * wide, -1, keepdims=True) + 1e-6)
-        ct = da[r, :].astype(BF).astype(F32)
-        back = scale * ct - wide * (scale * scale * scale * jnp.mean(wide * ct, -1, keepdims=True))
-        dh[r, :] = (dh[r, :].astype(F32) + back.astype(BF).astype(F32)).astype(BF)
-
-    start(silu_in(0, t) for t in range(TILES))
+        for i in range(TILE // 256):
+            r = pl.ds(pl.multiple_of(t * TILE + i * 256, 256), 256)
+            wide = h[r, :].astype(F32)
+            scale = lax.rsqrt(jnp.mean(wide * wide, -1, keepdims=True) + 1e-6)
+            ct = da[r, :].astype(BF).astype(F32)
+            back = scale * ct - wide * (scale * scale * scale * jnp.mean(wide * ct, -1, keepdims=True))
+            dh[r, :] = (dh[r, :].astype(F32) + back.astype(BF).astype(F32)).astype(BF)
+        silu_in(0, t).start()
+
     turned.wait()
 
 
@@ -313,7 +319,6 @@
                 silu_in(k + 1, t).start()
                 factor_in(k + 1, t).start()
 
-        finish(n - OWNS)
         gradients(n, (k + 1) % 2)
         sum_on_chip(n, 1)
 
@@ -367,7 +372,7 @@
             vmem((2 * CHUNKS, g_rows, C), BF), vmem((2 * CHUNKS, PIECE, D), BF),
             vmem((OWNS, g_rows, C), F32), vmem((OWNS, PIECE, D), F32),
             vmem((8, C), F32), vmem((8, D), F32), vmem((8, 128), F32), vmem((3, 8, 128), F32),
-            sem((3,)), sem((2, 12)), sem((2,)), sem((2, TILES)),
+            sem((3,)), sem((T // 256,)), sem((2, 12)), sem((2,)), sem((2, TILES)),
             sem((2, 2 * CHUNKS)), sem((2, 2 * CHUNKS)), sem((2, 2 * CHUNKS)), sem((2, 2 * CHUNKS)),
             sem((2 * CHUNKS, 9)), sem((3,)), sem((3,)),
         ],
@@ -382,12 +387,12 @@
     return list(pl.pallas_call(lambda *_: None, out_shape=[jax.ShapeDtypeStruct(s, BF) for s in shapes], out_specs=[space] * len(shapes), name="places")())
 
 
-def place_kernel(layer, which, part, _, out, tile, sem):
+def place_kernel(layer, which, first, part, _, out, tile, sem):
     me = lax.axis_index("dp")
     block = (me, me + 1 - 2 * (me % 2), (me + 2) % 4, 3 - me)[which]
     rows = part.shape[0] // 4
     ins = [pltpu.make_async_copy(part.at[pl.ds(i * rows, rows)], tile.at[pl.ds(i * rows, rows)], sem.at[0, i]) for i in range(4)]
-    outs = [pltpu.make_async_copy(tile.at[pl.ds(i * rows, rows)], out.at[layer, block, pl.ds(i * rows, rows)], sem.at[1, i]) for i in range(4)]
+    outs = [pltpu.make_async_copy(tile.at[pl.ds(i * rows, rows)], out.at[layer, block, pl.ds(first + i * rows, rows)], sem.at[1, i]) for i in range(4)]
     for c in ins:
         c.start()
     for i, o in zip(ins, outs, strict=True):
@@ -397,10 +402,10 @@
         c.wait()
 
 
-def place(out, part, layer, which):
+def place(out, part, layer, which, first):
     space = pl.BlockSpec(memory_space=pltpu.HBM)
     return pl.pallas_call(
-        functools.partial(place_kernel, layer, which),
+        functools.partial(place_kernel, layer, which, first),
         out_shape=jax.ShapeDtypeStruct(out.shape, out.dtype),
         in_specs=[ANY, space],
         out_specs=space,
@@ -426,7 +431,8 @@
             v = 0.95 * v + 0.05 * g * g
             return (w.astype(F32) - 0.02 * (m * lax.rsqrt(v + 1e-8) + 0.1 * w.astype(F32))).astype(BF), m, v
 
-        units = [(0, 0, 0, 112), (0, 0, 112, 112)] + [(i, layer, 0, gradients[i].shape[1]) for i in range(3) for layer in range(2)][1:]
+        units = [(0, 0, 0, 112), (0, 0, 112, 112)] + [(i, layer, 0, gradients[i].shape[1]) for i in range(3) for layer in range(2)][1:-1]
+        units += [(2, 1, 0, OWN_F // 2), (2, 1, OWN_F // 2, OWN_F // 2)]
         blocks = {}
         for u, (i, layer, first, rows) in enumerate(units):
             g = gradients[i]
@@ -443,7 +449,7 @@
             of_across = lax.ppermute(of_far, "dp", near)
             for which, part in enumerate((block, of_near, of_far, of_across)):
                 if i == 2:
-                    out[i] = place(out[i], part, layer, which)
+                    out[i] = place(out[i], part, layer, which, first)
                 else:
                     out[i] = lax.dynamic_update_slice(out[i], part[None, None], (layer, me ^ which, first, 0))
         new_w = [o.reshape(w.shape) for o, w in zip(out, weights, strict=True)]

time: 445 us -> 443 us (level)
  waiting for transfers between devices: 80.8 us -> 72.1 us
    ppermute x7 -> x8, waiting for transfers between devices: 80.7 us -> 71 us  [step(): of_far = lax.ppermute(block, 'dp', far)]
    pallas_call x8 -> x12, Pallas kernels: 16.3 us -> 23.1 us  [place(): pl.pallas_call(functools.partial(place_kernel, layer, which, first), out_...]
    convert_element_type x7 -> x8, other arithmetic: 25.5 us -> 27.7 us  [adamw(): (w.astype(F32) - 0.02 * (m * lax.rsqrt(v + 1e-08) + 0.1 * w.astype(F32)))...]
    ppermute x7 -> x8, starting transfers between devices: 10.5 us -> 10.2 us  [step(): of_far = lax.ppermute(block, 'dp', far)]
  transfers between devices with their start and end apart: 21 -> 24, of which waited for: 5 -> 6; matrix products, arithmetic and copies ran while one was open for 13% -> 14% of each run, Pallas kernels for 4% -> 5%
where the time goes in v3:
time: 443 us; the launch traced here: 442 us
  Pallas kernels  270 us (61%)
  waiting for transfers between devices  72.1 us (16%)
  other arithmetic  50.9 us (11%)
  local copies, waits for them, and re-layouts  35.1 us (8%)
  starting transfers between devices  12.7 us (3%)
    pallas_call x1, Pallas kernels, gradients_of(): pl.pallas_call(step_kernel, out_shape=[jax.ShapeDtypeStruct((2, OWN_D, FF...  247 us
    ppermute x8, waiting for transfers between devices, step(): of_far = lax.ppermute(block, 'dp', far)  71 us
    dynamic_update_slice x20, local copies, waits for them, and re-layouts, step(): lax.dynamic_update_slice(out[i], part[None, None], (layer, me ^ which, fi...  32.9 us
    convert_element_type x8, other arithmetic, adamw(): (w.astype(F32) - 0.02 * (m * lax.rsqrt(v + 1e-08) + 0.1 * w.astype(F32)))...  27.7 us
    add x2, other arithmetic, adamw(): v = 0.95 * v + 0.05 * g * g  23.2 us
    pallas_call x12, Pallas kernels, place(): pl.pallas_call(functools.partial(place_kernel, layer, which, first), out_...  23.1 us
    ppermute x8, starting transfers between devices, step(): of_far = lax.ppermute(block, 'dp', far)  10.2 us
  transfers between devices with their start and end apart: 24, of which 6 were waited for; matrix products, arithmetic and copies ran while one was open for 14% of the time, Pallas kernels for 5%

profile of v3, /device:TPU:0, one launch (start us, length us, event | category | flops | bytes accessed | tf_op | source)
XLA Modules:
  0.0 442.4 jit_solution(8750268360196043969)
XLA Ops:
  0.6 247.3 %gradients.1 = (bf16[2,224,2560]{2,1,0:T(8,128)(2,1)}, bf16[2,224,2560]{2,1,0:T(8,128)(2,1)}, bf16[2,640,896]{2,1,0:T(8,128)(2,1)}, f32[8,2560]{1,0:T(8,128)}, f...) custom-call(bf16[1,2048,896]{2,1,0:T(8,128)(2,1)} %x.1, ...), custom_call_target="tpu_custom_call" | custom-call | flops 140928614400 | bytes 200000000 | tf_op jit(solution)/shard_map/gradients/pallas_call | solution.py:351
  248.0 1.1 slice_reduce_fusion.5
  249.1 3.6 fusion.41
  252.7 3.4 fusion.44
  256.1 4.4 fusion.5
  260.7 4.1 fusion.8
  264.8 3.7 fusion.11
  268.6 2.6 fusion.14.part
  271.2 2.3 collective-permute-start.21
  273.7 0.3 collective-permute-start.1
  274.0 2.6 fusion.47.part
  276.7 3.4 fusion.50.part
  280.1 14.5 %fusion.1 = (f32[2,224,2560]{2,1,0:T(8,128)}, f32[2,224,2560]{2,1,0:T(8,128)}, f32[2,224,2560]{2,1,0:T(8,128)}, f32[2,224,2560]{2,1,0:T(8,128)}) fusion(f32[2,224,2560]{2,1,0:T(8,128)} %param.20, bf16[2,224,2560]{2,1,0:T(8,128)(2,1)} %get-tuple-element.41, f32[2560]{0:T(1024)S(1)} %slice_reduce_fusion, f32[2,224,2560]{2,1,0:T(8,128)} %param.17, ...), kind=kLoop, calls=%fused_computation.4 | loop fusion | flops 20643840 | bytes 41297920 | tf_op jit(solution)/shard_map/add | solution.py:431
  294.6 2.2 place.12._
  296.8 8.7 %fusion.2 = (f32[2,640,896]{2,1,0:T(8,128)}, f32[2,640,896]{2,1,0:T(8,128)}) fusion(f32[2,640,896]{2,1,0:T(8,128)} %param.21, bf16[2,640,896]{2,1,0:T(8,128)(2,1)S(1)} %copy-done.4, f32[896]{0:T(1024)S(1)} %slice_reduce_fusion.6, f32[2,640,896]{2,1,0:T(8,128)} %param.18), kind=kLoop, calls=%fused_computation.5 | loop fusion | flops 10321920 | bytes 20647424 | tf_op jit(solution)/shard_map/add | solution.py:431
  305.5 2.3 bitcast_dynamic-update-slice_fusion.7
  307.9 1.9 bitcast_dynamic-update-slice_fusion.19
  309.8 1.7 collective-permute-start.18
  311.5 0.3 collective-permute-done.1
  311.8 1.9 bitcast_dynamic-update-slice_fusion.18
  313.7 1.9 bitcast_dynamic-update-slice_fusion.17
  315.6 0.5 collective-permute-start.9
  316.1 2.0 place.13._
  318.2 2.0 place.14._
  320.3 1.8 collective-permute-start.4
  322.0 0.8 bitcast_dynamic-update-slice_fusion.16
  322.9 0.8 bitcast_dynamic-update-slice_fusion.15
  323.7 0.3 collective-permute-start.10
  324.0 14.1 %collective-permute-done.4 = bf16[112,2560]{1,0:T(8,128)(2,1)S(1)} collective-permute-done((bf16[112,2560]{1,0:T(8,128)(2,1)S(1)}, bf16[112,2560]{1,0:T(8,128)(2,1)S(1)}, u32[]{:S(2)}, u32[]{:S(2)}) %collective-permute-start.4) | collective-permute-done | bytes 573472 | tf_op jit(solution)/shard_map/ppermute | solution.py:447
  338.1 0.8 bitcast_dynamic-update-slice_fusion.14
  339.0 0.8 bitcast_dynamic-update-slice_fusion.13
  339.8 0.3 collective-permute-done.5
  340.3 0.8 bitcast_dynamic-update-slice_fusion.12
  341.2 1.1 bitcast_dynamic-update-slice_fusion.11
  342.3 0.9 collective-permute-done.22.part
  343.1 0.2 collective-permute-start.6
  343.3 0.8 copy-done.11
  344.1 2.0 place.15._
  346.2 1.8 collective-permute-start.7
  347.9 2.3 bitcast_dynamic-update-slice_fusion.6
  350.3 1.9 place.16._
  352.2 1.9 place.17._
  354.2 0.3 collective-permute-start.13
  354.5 8.3 %collective-permute-done.10 = bf16[224,2560]{1,0:T(8,128)(2,1)} collective-permute-done((bf16[224,2560]{1,0:T(8,128)(2,1)}, bf16[224,2560]{1,0:T(8,128)(2,1)}, u32[]{:S(2)}, u32[]{:S(2)}) %collective-permute-start.10) | collective-permute-done | bytes 1146912 | tf_op jit(solution)/shard_map/ppermute | solution.py:447
  362.8 2.3 bitcast_dynamic-update-slice_fusion.5
  365.1 1.8 place.18._
  367.0 1.8 collective-permute-start.15
  368.8 1.8 place.19._
  370.6 0.2 collective-permute-start.11
  370.9 2.3 bitcast_dynamic-update-slice_fusion.10
  373.2 1.8 place.20._
  375.1 0.3 collective-permute-start.12
  375.4 48.3 %collective-permute-done.15.part = bf16[320,896]{1,0:T(8,128)(2,1)} collective-permute-done((bf16[320,896]{1,0:T(8,128)(2,1)S(1)}, bf16[320,896]{1,0:T(8,128)(2,1)}, u32[]{:S(2)}, u32[]{:S(2)}) %collective-permute-start.15) | collective-permute-done | bytes 573472 | tf_op jit(solution)/shard_map/ppermute | solution.py:447
  423.7 0.5 collective-permute-start.14
  424.2 1.8 place.21._
  426.1 2.3 bitcast_dynamic-update-slice_fusion.9
  428.4 1.8 place.22._
  430.3 1.8 place.23
  432.1 2.3 bitcast_dynamic-update-slice_fusion.4
  434.5 1.1 bitcast_dynamic-update-slice_fusion.3
  435.6 2.3 bitcast_dynamic-update-slice_fusion.2
  437.9 2.3 bitcast_dynamic-update-slice_fusion.1
  440.2 1.1 bitcast_dynamic-update-slice_fusion
  441.3 1.1 bitcast_dynamic-update-slice_fusion.8
  (81 shorter events, 1.0 us)
Async XLA Ops:
  248.0 4.7 %copy-start.13 = (f32[8,2560]{1,0:T(8,128)S(1)}, f32[8,2560]{1,0:T(8,128)}, u32[]{:S(2)}) copy-start(f32[8,2560]{1,0:T(8,128)} %get-tuple-element.54) | copy-start | bytes 245764
  248.0 4.7 %copy-start.2 = (bf16[2,224,2560]{2,1,0:T(8,128)(2,1)S(1)}, bf16[2,224,2560]{2,1,0:T(8,128)(2,1)}, u32[]{:S(2)}) copy-start(bf16[2,224,2560]{2,1,0:T(8,128)(2,1)} %get-tuple-element.33) | copy-start | bytes 6881284
  249.0 7.0 %copy-start = (f32[2,224,2560]{2,1,0:T(8,128)S(1)}, f32[2,224,2560]{2,1,0:T(8,128)}, u32[]{:S(2)}) copy-start(f32[2,224,2560]{2,1,0:T(8,128)} %param.19) | copy-start | bytes 13762564
  252.7 7.9 %slice-start = ((s8[4587520]{0:T(1024)(128)(4,1)}), s8[4194304]{0:T(1024)(128)(4,1)S(1)}, s32[]{:S(2)}) async-start(s8[4587520]{0:T(1024)(128)(4,1)} %bitcast.127), calls=%async_computation | async-start | bytes 8388608
  256.1 4.5 %slice-start.1 = ((s8[4587520]{0:T(1024)(128)(4,1)}), s8[393216]{0:T(1024)(128)(4,1)S(1)}, s32[]{:S(2)}) async-start(s8[4587520]{0:T(1024)(128)(4,1)} %bitcast.127), calls=%async_computation.1 | async-start | bytes 786432
  256.1 4.5 %copy-start.1 = (f32[2,224,2560]{2,1,0:T(8,128)S(1)}, f32[2,224,2560]{2,1,0:T(8,128)}, u32[]{:S(2)}) copy-start(f32[2,224,2560]{2,1,0:T(8,128)} %param.17) | copy-start | bytes 13762564
  256.1 8.7 %copy-start.5 = (bf16[2,224,2560]{2,1,0:T(8,128)(2,1)S(1)}, bf16[2,224,2560]{2,1,0:T(8,128)(2,1)}, u32[]{:S(2)}) copy-start(bf16[2,224,2560]{2,1,0:T(8,128)(2,1)} %get-tuple-element.41) | copy-start | bytes 6881284
  260.6 7.9 %slice-start.2 = ((s8[4587520]{0:T(1024)(128)(4,1)}), s8[4194304]{0:T(1024)(128)(4,1)S(1)}, s32[]{:S(2)}) async-start(s8[4587520]{0:T(1024)(128)(4,1)} %bitcast.129), calls=%async_computation.2 | async-start | bytes 8388608
  260.6 7.9 %slice-start.4 = ((s8[4587520]{0:T(1024)(128)(4,1)}), s8[4194304]{0:T(1024)(128)(4,1)S(1)}, s32[]{:S(2)}) async-start(s8[4587520]{0:T(1024)(128)(4,1)} %bitcast.131), calls=%async_computation.4 | async-start | bytes 8388608
  264.7 3.8 slice-start.3
  264.7 3.8 slice-start.5
  264.8 3.8 copy-start.3
  271.2 8.9 %copy-start.6 = (bf16[640,896]{1,0:T(8,128)(2,1)}, bf16[640,896]{1,0:T(8,128)(2,1)S(1)}, u32[]{:S(2)}) copy-start(bf16[640,896]{1,0:T(8,128)(2,1)S(1)} %fusion.14.part) | copy-start | bytes 3440644
  271.2 44.4 %collective-permute-start.23 = (bf16[640,896]{1,0:T(8,128)(2,1)S(1)}, bf16[640,896]{1,0:T(8,128)(2,1)}, u32[]{:S(2)}, u32[]{:S(2)}) collective-permute-start(bf16[640,896]{1,0:T(8,128)(2,1)S(1)} %fusion.14.part), channel_id=1, source_target_pairs={{0,1},{1,0},{2,3},{3,2},{4,5},{5,4},{6,7},{7,6}} | collective-permute-start | bytes 3440648 | tf_op jit(solution)/shard_map/ppermute | solution.py:448
  271.2 46.9 %collective-permute-start.21 = (bf16[640,896]{1,0:T(8,128)(2,1)S(1)}, bf16[640,896]{1,0:T(8,128)(2,1)}, u32[]{:S(2)}, u32[]{:S(2)}) collective-permute-start(bf16[640,896]{1,0:T(8,128)(2,1)S(1)} %fusion.14.part), channel_id=1, source_target_pairs={{0,2},{1,3},{2,0},{3,1},{4,6},{5,7},{6,4},{7,5}} | collective-permute-start | bytes 3440648 | tf_op jit(solution)/shard_map/ppermute | solution.py:447
  273.6 36.2 %collective-permute-start = (bf16[112,2560]{1,0:T(8,128)(2,1)}, bf16[112,2560]{1,0:T(8,128)(2,1)}, u32[]{:S(2)}, u32[]{:S(2)}) collective-permute-start(bf16[112,2560]{1,0:T(8,128)(2,1)} %fusion.41), channel_id=1, source_target_pairs={{0,1},{1,0},{2,3},{3,2},{4,5},{5,4},{6,7},{7,6}} | collective-permute-start | bytes 1720328 | tf_op jit(solution)/shard_map/ppermute | solution.py:448
  273.7 38.1 %collective-permute-start.1 = (bf16[112,2560]{1,0:T(8,128)(2,1)}, bf16[112,2560]{1,0:T(8,128)(2,1)}, u32[]{:S(2)}, u32[]{:S(2)}) collective-permute-start(bf16[112,2560]{1,0:T(8,128)(2,1)} %fusion.41), channel_id=1, source_target_pairs={{0,2},{1,3},{2,0},{3,1},{4,6},{5,7},{6,4},{7,5}} | collective-permute-start | bytes 1720328 | tf_op jit(solution)/shard_map/ppermute | solution.py:447
  276.6 75.6 %collective-permute-start.20 = (bf16[320,896]{1,0:T(8,128)(2,1)}, bf16[320,896]{1,0:T(8,128)(2,1)}, u32[]{:S(2)}, u32[]{:S(2)}) collective-permute-start(bf16[320,896]{1,0:T(8,128)(2,1)} %fusion.47.part), channel_id=1, source_target_pairs={{0,1},{1,0},{2,3},{3,2},{4,5},{5,4},{6,7},{7,6}} | collective-permute-start | bytes 1720328 | tf_op jit(solution)/shard_map/ppermute | solution.py:448
  294.6 2.2 copy-start.4
  309.8 44.4 %collective-permute-start.18 = (bf16[320,896]{1,0:T(8,128)(2,1)}, bf16[320,896]{1,0:T(8,128)(2,1)}, u32[]{:S(2)}, u32[]{:S(2)}) collective-permute-start(bf16[320,896]{1,0:T(8,128)(2,1)} %fusion.47.part), channel_id=1, source_target_pairs={{0,2},{1,3},{2,0},{3,1},{4,6},{5,7},{6,4},{7,5}} | collective-permute-start | bytes 1720328 | tf_op jit(solution)/shard_map/ppermute | solution.py:447
  311.8 8.5 %collective-permute-start.2 = (bf16[112,2560]{1,0:T(8,128)(2,1)}, bf16[112,2560]{1,0:T(8,128)(2,1)S(1)}, u32[]{:S(2)}, u32[]{:S(2)}) collective-permute-start(bf16[112,2560]{1,0:T(8,128)(2,1)} %collective-permute-done.1), channel_id=1, source_target_pairs={{0,1},{1,0},{2,3},{3,2},{4,5},{5,4},{6,7},{7,6}} | collective-permute-start | bytes 1720328 | tf_op jit(solution)/shard_map/ppermute | solution.py:449
  315.6 2.6 copy-start.9
  315.6 30.6 %collective-permute-start.9 = (bf16[224,2560]{1,0:T(8,128)(2,1)}, bf16[224,2560]{1,0:T(8,128)(2,1)}, u32[]{:S(2)}, u32[]{:S(2)}) collective-permute-start(bf16[224,2560]{1,0:T(8,128)(2,1)} %fusion.8), channel_id=1, source_target_pairs={{0,1},{1,0},{2,3},{3,2},{4,5},{5,4},{6,7},{7,6}} | collective-permute-start | bytes 3440648 | tf_op jit(solution)/shard_map/ppermute | solution.py:448
  318.2 5.6 %collective-permute-start.3 = (bf16[112,2560]{1,0:T(8,128)(2,1)S(1)}, bf16[112,2560]{1,0:T(8,128)(2,1)S(1)}, u32[]{:S(2)}, u32[]{:S(2)}) collective-permute-start(bf16[112,2560]{1,0:T(8,128)(2,1)S(1)} %copy-done.9), channel_id=1, source_target_pairs={{0,1},{1,0},{2,3},{3,2},{4,5},{5,4},{6,7},{7,6}} | collective-permute-start | bytes 1720328 | tf_op jit(solution)/shard_map/ppermute | solution.py:448
  320.3 17.8 %collective-permute-start.4 = (bf16[112,2560]{1,0:T(8,128)(2,1)S(1)}, bf16[112,2560]{1,0:T(8,128)(2,1)S(1)}, u32[]{:S(2)}, u32[]{:S(2)}) collective-permute-start(bf16[112,2560]{1,0:T(8,128)(2,1)S(1)} %copy-done.9), channel_id=1, source_target_pairs={{0,2},{1,3},{2,0},{3,1},{4,6},{5,7},{6,4},{7,5}} | collective-permute-start | bytes 1720328 | tf_op jit(solution)/shard_map/ppermute | solution.py:447
  322.9 18.3 %copy-start.8 = (bf16[224,2560]{1,0:T(8,128)(2,1)S(1)}, bf16[224,2560]{1,0:T(8,128)(2,1)}, u32[]{:S(2)}) copy-start(bf16[224,2560]{1,0:T(8,128)(2,1)} %fusion.5) | copy-start | bytes 3440644
  323.7 39.1 %collective-permute-start.10 = (bf16[224,2560]{1,0:T(8,128)(2,1)}, bf16[224,2560]{1,0:T(8,128)(2,1)}, u32[]{:S(2)}, u32[]{:S(2)}) collective-permute-start(bf16[224,2560]{1,0:T(8,128)(2,1)} %fusion.8), channel_id=1, source_target_pairs={{0,2},{1,3},{2,0},{3,1},{4,6},{5,7},{6,4},{7,5}} | collective-permute-start | bytes 3440648 | tf_op jit(solution)/shard_map/ppermute | solution.py:447
  338.1 2.0 collective-permute-start.5
  340.1 3.0 collective-permute-start.22
  343.1 1.0 copy-start.11
  343.1 27.5 %collective-permute-start.6 = (bf16[224,2560]{1,0:T(8,128)(2,1)S(1)}, bf16[224,2560]{1,0:T(8,128)(2,1)}, u32[]{:S(2)}, u32[]{:S(2)}) collective-permute-start(bf16[224,2560]{1,0:T(8,128)(2,1)S(1)} %copy-done.8), channel_id=1, source_target_pairs={{0,1},{1,0},{2,3},{3,2},{4,5},{5,4},{6,7},{7,6}} | collective-permute-start | bytes 3440648 | tf_op jit(solution)/shard_map/ppermute | solution.py:448
  346.2 78.0 %collective-permute-start.7 = (bf16[224,2560]{1,0:T(8,128)(2,1)S(1)}, bf16[224,2560]{1,0:T(8,128)(2,1)}, u32[]{:S(2)}, u32[]{:S(2)}) collective-permute-start(bf16[224,2560]{1,0:T(8,128)(2,1)S(1)} %copy-done.8), channel_id=1, source_target_pairs={{0,2},{1,3},{2,0},{3,1},{4,6},{5,7},{6,4},{7,5}} | collective-permute-start | bytes 3440648 | tf_op jit(solution)/shard_map/ppermute | solution.py:447
  350.3 1.9 copy-start.10
  352.2 2.0 copy-start.7
  352.2 22.8 %collective-permute-start.17 = (bf16[320,896]{1,0:T(8,128)(2,1)S(1)}, bf16[320,896]{1,0:T(8,128)(2,1)S(1)}, u32[]{:S(2)}, u32[]{:S(2)}) collective-permute-start(bf16[320,896]{1,0:T(8,128)(2,1)S(1)} %copy-done.10), channel_id=1, source_target_pairs={{0,1},{1,0},{2,3},{3,2},{4,5},{5,4},{6,7},{7,6}} | collective-permute-start | bytes 1720328 | tf_op jit(solution)/shard_map/ppermute | solution.py:448
  354.2 69.5 %collective-permute-start.13 = (bf16[224,2560]{1,0:T(8,128)(2,1)S(1)}, bf16[224,2560]{1,0:T(8,128)(2,1)}, u32[]{:S(2)}, u32[]{:S(2)}) collective-permute-start(bf16[224,2560]{1,0:T(8,128)(2,1)S(1)} %copy-done.7), channel_id=1, source_target_pairs={{0,2},{1,3},{2,0},{3,1},{4,6},{5,7},{6,4},{7,5}} | collective-permute-start | bytes 3440648 | tf_op jit(solution)/shard_map/ppermute | solution.py:447
  362.8 4.2 collective-permute-start.19
  367.0 56.7 %collective-permute-start.15 = (bf16[320,896]{1,0:T(8,128)(2,1)S(1)}, bf16[320,896]{1,0:T(8,128)(2,1)}, u32[]{:S(2)}, u32[]{:S(2)}) collective-permute-start(bf16[320,896]{1,0:T(8,128)(2,1)S(1)} %copy-done.10), channel_id=1, source_target_pairs={{0,2},{1,3},{2,0},{3,1},{4,6},{5,7},{6,4},{7,5}} | collective-permute-start | bytes 1720328 | tf_op jit(solution)/shard_map/ppermute | solution.py:447
  370.6 61.5 %collective-permute-start.11 = (bf16[224,2560]{1,0:T(8,128)(2,1)}, bf16[224,2560]{1,0:T(8,128)(2,1)}, u32[]{:S(2)}, u32[]{:S(2)}) collective-permute-start(bf16[224,2560]{1,0:T(8,128)(2,1)} %collective-permute-done.10), channel_id=1, source_target_pairs={{0,1},{1,0},{2,3},{3,2},{4,5},{5,4},{6,7},{7,6}} | collective-permute-start | bytes 3440648 | tf_op jit(solution)/shard_map/ppermute | solution.py:449
  375.1 48.6 %copy-start.12 = (bf16[320,896]{1,0:T(8,128)(2,1)}, bf16[320,896]{1,0:T(8,128)(2,1)S(1)}, u32[]{:S(2)}) copy-start(bf16[320,896]{1,0:T(8,128)(2,1)S(1)} %collective-permute-done.17.part) | copy-start | bytes 1720324
  375.1 60.5 %collective-permute-start.12 = (bf16[224,2560]{1,0:T(8,128)(2,1)S(1)}, bf16[224,2560]{1,0:T(8,128)(2,1)}, u32[]{:S(2)}, u32[]{:S(2)}) collective-permute-start(bf16[224,2560]{1,0:T(8,128)(2,1)S(1)} %copy-done.7), channel_id=1, source_target_pairs={{0,1},{1,0},{2,3},{3,2},{4,5},{5,4},{6,7},{7,6}} | collective-permute-start | bytes 3440648 | tf_op jit(solution)/shard_map/ppermute | solution.py:448
  423.7 6.6 %collective-permute-start.16 = (bf16[320,896]{1,0:T(8,128)(2,1)}, bf16[320,896]{1,0:T(8,128)(2,1)}, u32[]{:S(2)}, u32[]{:S(2)}) collective-permute-start(bf16[320,896]{1,0:T(8,128)(2,1)} %collective-permute-done.15.part), channel_id=1, source_target_pairs={{0,1},{1,0},{2,3},{3,2},{4,5},{5,4},{6,7},{7,6}} | collective-permute-start | bytes 1720328 | tf_op jit(solution)/shard_map/ppermute | solution.py:449
  423.7 16.6 %collective-permute-start.14 = (bf16[224,2560]{1,0:T(8,128)(2,1)}, bf16[224,2560]{1,0:T(8,128)(2,1)S(1)}, u32[]{:S(2)}, u32[]{:S(2)}) collective-permute-start(bf16[224,2560]{1,0:T(8,128)(2,1)} %collective-permute-done.13), channel_id=1, source_target_pairs={{0,1},{1,0},{2,3},{3,2},{4,5},{5,4},{6,7},{7,6}} | collective-permute-start | bytes 3440648 | tf_op jit(solution)/shard_map/ppermute | solution.py:449
  424.2 17.1 %collective-permute-start.8 = (bf16[224,2560]{1,0:T(8,128)(2,1)}, bf16[224,2560]{1,0:T(8,128)(2,1)S(1)}, u32[]{:S(2)}, u32[]{:S(2)}) collective-permute-start(bf16[224,2560]{1,0:T(8,128)(2,1)} %collective-permute-done.7), channel_id=1, source_target_pairs={{0,1},{1,0},{2,3},{3,2},{4,5},{5,4},{6,7},{7,6}} | collective-permute-start | bytes 3440648 | tf_op jit(solution)/shard_map/ppermute | solution.py:449
